TPU v7x, 128 devices: a whole 4x4x4 slice. The times are simulated.
128 devices in a mesh: sub: 2 (over core), fsdp: 64 (over z, y, x).
Axes of the slice: x: 4, y: 4, z: 4, core: 2. Of those that a mesh axis runs over, the one named last changes fastest.
Arguments:
- x_in: bfloat16 [131072, 1024], P(('sub', 'fsdp'))
- w_up: bfloat16 [1, 1024, 4096], P(None, ('sub', 'fsdp'))
- w_down: bfloat16 [1, 4096, 1024], P(None, ('sub', 'fsdp'))
- grad_out: bfloat16 [131072, 1024], P(('sub', 'fsdp'))
Outputs:
- output 1: bfloat16 [131072, 1024], P(('sub', 'fsdp'))
- output 2: bfloat16 [131072, 1024], P(('sub', 'fsdp'))
- output 3: float32 [1, 1024, 4096], P(None, ('sub', 'fsdp'))
- output 4: float32 [1, 4096, 1024], P(None, ('sub', 'fsdp'))
All inputs are finite; a program needn't handle non-finite values.
Results may differ from a plain program's by a relative error of at most 0.001.
Values are sent between devices in bfloat16 or wider.
A program may use at most 1 GiB of HBM per device.

v0:
```python
import jax
import jax.numpy as jnp
from jax import lax
from jax.sharding import PartitionSpec as P

SHARD_AXES = ("sub", "fsdp")
CONTRACT_LAST = (((1,), (1,)), ((), ()))
CONTRACT_FIRST = (((0,), (0,)), ((), ()))


def solution(mesh):
    def local_stack(x_loc, up_loc, down_loc, grad_loc):
        n_layers = up_loc.shape[0]
        hidden = x_loc
        saved_inputs = []
        for layer_idx in range(n_layers):
            up_full = lax.all_gather(up_loc[layer_idx], SHARD_AXES, axis=0, tiled=True)
            down_full = lax.all_gather(down_loc[layer_idx], SHARD_AXES, axis=0, tiled=True)
            saved_inputs.append(hidden)
            pre_act = jnp.dot(hidden, up_full, preferred_element_type=jnp.float32)
            act_bf = jax.nn.gelu(pre_act).astype(jnp.bfloat16)
            branch = jnp.dot(act_bf, down_full, preferred_element_type=jnp.float32)
            hidden = (hidden.astype(jnp.float32) + branch).astype(jnp.bfloat16)
        grad_now = grad_loc
        up_grads = []
        down_grads = []
        for layer_idx in reversed(range(n_layers)):
            up_full = lax.all_gather(up_loc[layer_idx], SHARD_AXES, axis=0, tiled=True)
            down_full = lax.all_gather(down_loc[layer_idx], SHARD_AXES, axis=0, tiled=True)
            layer_in = saved_inputs[layer_idx]
            pre_act = jnp.dot(layer_in, up_full, preferred_element_type=jnp.float32)
            act_f32, gelu_back = jax.vjp(jax.nn.gelu, pre_act)
            act_bf = act_f32.astype(jnp.bfloat16)
            d_act = lax.dot_general(grad_now, down_full, CONTRACT_LAST, preferred_element_type=jnp.float32)
            d_pre = gelu_back(d_act)[0].astype(jnp.bfloat16)
            down_part = lax.dot_general(act_bf, grad_now, CONTRACT_FIRST, preferred_element_type=jnp.float32)
            up_part = lax.dot_general(layer_in, d_pre, CONTRACT_FIRST, preferred_element_type=jnp.float32)
            back_branch = lax.dot_general(d_pre, up_full, CONTRACT_LAST, preferred_element_type=jnp.float32)
            grad_now = (grad_now.astype(jnp.float32) + back_branch).astype(jnp.bfloat16)
            up_grads.append(lax.psum_scatter(up_part, SHARD_AXES, scatter_dimension=0, tiled=True))
            down_grads.append(lax.psum_scatter(down_part, SHARD_AXES, scatter_dimension=0, tiled=True))
        return hidden, grad_now, jnp.stack(up_grads[::-1]), jnp.stack(down_grads[::-1])

    tok_spec = P(SHARD_AXES, None)
    mat_spec = P(None, SHARD_AXES, None)
    return jax.shard_map(local_stack, mesh=mesh, in_specs=(tok_spec, mat_spec, mat_spec, tok_spec), out_specs=(tok_spec, tok_spec, mat_spec, mat_spec), check_vma=False)
```

profile of v0, /device:TPU:1, one launch (start us, length us, event | category | flops | bytes accessed | tf_op | source)
XLA Modules:
  0.0 1597.0 jit_solution(9342726447845089776)
XLA Ops:
  7.2 0.0 all-gather.5.cloned.1.call-start
  7.2 0.7 all-gather.5.cloned.1.call-update
  7.9 0.0 all-gather.7.cloned.1.call-start
  7.9 0.7 all-gather.7.cloned.1.call-update
  8.7 0.0 copy-start
  8.7 0.0 reduce-scatter.7.cloned.1.call-start
  8.7 75.6 %all-gather.5.cloned.1.call-done = bf16[1,1024,4096]{2,1,0:T(8,128)(2,1)} async-done(((bf16[1,8,4096]{2,1,0:T(8,128)(2,1)}), bf16[1,1024,4096]{2,1,0:T(8,128)(2,1)}) %all-gather.5.cloned.1.call-update) | async-done | bytes 8388624 | tf_op jit(solution)/shard_map/all_gather | solution.py:17
  84.3 16.0 %fusion.13 = f32[1024,4096]{1,0:T(8,128)} fusion(bf16[1024,1024]{1,0:T(8,128)(2,1)} %param.4, bf16[1,1024,4096]{2,1,0:T(8,128)(2,1)} %all-gather.5.cloned.1.call-done), kind=kOutput, calls=%fused_computation.17 | convolution fusion | flops 8589934592 | bytes 27262976 | tf_op jit(solution)/shard_map/dot_general | solution.py:20
  100.3 54.4 %all-gather.7.cloned.1.call-done = bf16[1,4096,1024]{2,1,0:T(8,128)(2,1)} async-done(((bf16[1,32,1024]{2,1,0:T(8,128)(2,1)}), bf16[1,4096,1024]{2,1,0:T(8,128)(2,1)}) %all-gather.7.cloned.1.call-update) | async-done | bytes 8388624 | tf_op jit(solution)/shard_map/all_gather | solution.py:18
  154.7 0.0 copy-done
  154.7 22.8 %fusion.6 = bf16[1024,4096]{1,0:T(8,128)(2,1)} fusion(f32[1024,4096]{1,0:T(8,128)} %fusion.13, bf16[1024,1024]{1,0:T(8,128)(2,1)S(1)} %copy-done, bf16[1,4096,1024]{2,1,0:T(8,128)(2,1)} %all-gather.7.cloned.1.call-done), kind=kOutput, calls=%fused_computation.8 | convolution fusion | flops 8673820672 | bytes 35651584 | tf_op jit(solution)/shard_map/dot_general | solution.py:34
  177.5 16.2 %convolution_bitcast_fusion = f32[1024,4096]{0,1:T(8,128)} fusion(bf16[1024,4096]{1,0:T(8,128)(2,1)} %fusion.6, bf16[1024,1024]{1,0:T(8,128)(2,1)} %param.4), kind=kOutput, calls=%fused_computation.10 | convolution fusion | flops 8589934592 | bytes 27262976 | tf_op jit(solution)/shard_map/dot_general | solution.py:37
  193.6 17.5 %copy.10 = f32[1024,4096]{1,0:T(8,128)} copy(f32[1024,4096]{0,1:T(8,128)} %convolution_bitcast_fusion) | data formatting | bytes 33554432
  211.1 0.0 reduce-scatter.7.cloned.1.call-update
  211.2 0.0 reduce-scatter.5.cloned.1.call-start
  211.2 18.5 %fusion.21 = f32[4096,1024]{1,0:T(8,128)} fusion(bf16[1024,1024]{1,0:T(8,128)(2,1)S(1)} %copy-done, f32[1024,4096]{1,0:T(8,128)} %fusion.13), kind=kOutput, calls=%fused_computation.21 | convolution fusion | flops 8627683328 | bytes 35651584 | tf_op jit(solution)/shard_map/dot_general | solution.py:36
  229.7 0.0 reduce-scatter.5.cloned.1.call-update
  229.7 0.0 copy-start.1
  229.7 14.8 add_convert_fusion
  244.6 0.0 copy-done.1
  244.6 17.1 %add_convert_fusion.1 = bf16[1024,1024]{1,0:T(8,128)(2,1)} fusion(bf16[1024,1024]{1,0:T(8,128)(2,1)S(1)} %copy-done.1, bf16[1,4096,1024]{2,1,0:T(8,128)(2,1)} %all-gather.7.cloned.1.call-done, f32[1024,4096]{1,0:T(8,128)} %fusion.13), kind=kOutput, calls=%fused_computation.20 | convolution fusion | flops 8630829056 | bytes 29360128 | tf_op jit(solution)/shard_map/dot_general | solution.py:22
  261.7 637.9 %reduce-scatter.7.cloned.1.call-done = f32[8,4096]{1,0:T(8,128)} async-done(((f32[1024,4096]{1,0:T(8,128)}), f32[8,4096]{1,0:T(8,128)}) %reduce-scatter.7.cloned.1.call-update) | async-done | bytes 131088
  899.6 1.5 copy.11
  901.1 1.2 copy.9
  902.3 688.2 %reduce-scatter.5.cloned.1.call-done = f32[32,1024]{1,0:T(8,128)} async-done(((f32[4096,1024]{1,0:T(8,128)}), f32[32,1024]{1,0:T(8,128)}) %reduce-scatter.5.cloned.1.call-update) | async-done | bytes 131088 | tf_op jit(solution)/shard_map/reduce_scatter | solution.py:41
Async XLA Ops:
  7.2 77.1 %all-gather.5.cloned.1.call-start = ((), (), s32[]{:S(2)}) async-start(), calls=%async_computation.3 | async-start | bytes 8454144 | tf_op jit(solution)/shard_map/all_gather | solution.py:17
  7.9 146.8 %all-gather.7.cloned.1.call-start = ((), (), s32[]{:S(2)}) async-start(), calls=%async_computation.4 | async-start | bytes 8454144 | tf_op jit(solution)/shard_map/all_gather | solution.py:18
  8.7 146.0 %copy-start = (bf16[1024,1024]{1,0:T(8,128)(2,1)S(1)}, bf16[1024,1024]{1,0:T(8,128)(2,1)}, u32[]{:S(2)}) copy-start(bf16[1024,1024]{1,0:T(8,128)(2,1)} %param.7) | copy-start | bytes 6291460
  8.7 890.9 %reduce-scatter.7.cloned.1.call-start = ((), (), s32[]{:S(2)}) async-start(), calls=%async_computation.5 | async-start | bytes 16908288
  211.2 1379.3 %reduce-scatter.5.cloned.1.call-start = ((), (), s32[]{:S(2)}) async-start(), calls=%async_computation.2 | async-start | bytes 16908288 | tf_op jit(solution)/shard_map/reduce_scatter | solution.py:41
  229.7 14.9 copy-start.1
Sparse Core Ops, SparseCore 0:
  11.1 73.1 all-gather.4
  87.4 67.1 all-gather.6
  211.3 688.2 reduce-scatter.6
  902.4 688.0 reduce-scatter.4
where the time goes:
time: 1600 us
  waiting for transfers between devices  1460 us (91%)
  matrix products  105 us (7%)
  local copies, waits for them, and re-layouts  20.2 us (1%)
    reduce_scatter x1, waiting for transfers between devices, local_stack(): lax.psum_scatter(down_part, SHARD_AXES, scatter_dimension=0, tiled=True)  688 us
    unnamed x5, waiting for transfers between devices  639 us
    all_gather x1, waiting for transfers between devices, local_stack(): up_full = lax.all_gather(up_loc[layer_idx], SHARD_AXES, axis=0, tiled=True)  75.6 us
    all_gather x1, waiting for transfers between devices, local_stack(): lax.all_gather(down_loc[layer_idx], SHARD_AXES, axis=0, tiled=True)  54.4 us
  transfers between devices with their start and end apart: 4, of which 4 were waited for; matrix products, arithmetic and copies ran while one was open for 4% of the time, Pallas kernels for 0%

commit v1 on v0

v1 whole, which is shorter than its diff:
```python
import jax
import jax.numpy as jnp
from jax import lax
from jax.experimental import pallas as pl
from jax.experimental.pallas import tpu as pltpu
from jax.sharding import PartitionSpec as P

f32, bf16 = jnp.float32, jnp.bfloat16
MESH = pl.DeviceIdType.MESH
NN, NT, TN = [(((i,), (k,)), ((), ())) for i, k in ((1, 0), (1, 1), (0, 0))]
ANY = pl.BlockSpec(memory_space=pl.ANY)
VMEM = pl.BlockSpec(memory_space=pltpu.VMEM)
AXES = ("sub", "fsdp")

TOK = 1024
DIM = 1024
HALF = 2048
R = 4
SUBL, LANE = 8, 128
COL = 256
CHUNKS = HALF // COL
STEP = 512
STEPS = 2 * TOK // STEP
U2 = 16
SLOTS = 3
ROUNDS = (11, 11, 10)
CLASSES = DIMS = range(3)
PAIRS = ((0, 1), (2,))
BOTH = range(2)
ORDERS = ((0, 1, 2), (1, 2, 0), (2, 0, 1))
STRIDE = (R * R, R, 1)
C0 = 0.7978845608028654
C1 = 0.044715 * C0
ALL = slice(None)

W1_LANES = ((0, COL, 3), (3 * COL, COL, 3), (6 * COL, COL, 2))
W2_LANES = ((0, COL, 1), (COL, COL, 1), (2 * COL, 2 * COL, 1))


def dot(a, b, dims):
    return lax.dot_general(a, b, dims, preferred_element_type=f32)


def span(i, n):
    return pl.ds(pl.multiple_of(i * n, n), n)


class Place:
    def __init__(self):
        self.s, self.j = lax.axis_index("sub"), lax.axis_index("fsdp")
        self.c = [lax.rem(lax.div(self.j, n), R) for n in STRIDE]
        self.plus, self.minus, self.opp = [[lax.rem(c + o, R) for c in self.c] for o in (1, 3, 2)]
        self.partner = (1 - self.s, self.j)

    def dev(self, d, v):
        return (self.s, self.j + (v - self.c[d]) * STRIDE[d])

    def near(self, d, dirn):
        return self.minus[d] if dirn else self.plus[d]

    def others(self, d):
        return self.plus[d], self.minus[d], self.opp[d]


def remote(src, dst, ssem, rsem, dev):
    return pltpu.make_async_remote_copy(src, dst, ssem, rsem, device_id=dev, device_id_type=MESH)


def arrived(ref, sem):
    pltpu.make_async_copy(ref, ref, sem).wait()


def part(half, n=2):
    return ALL if half is None else pl.ds(half * n, n)


class Gather:
    def __init__(self, pc, w, lead, lanes, sems, base):
        self.pc, self.w, self.lead, self.lanes = pc, w, lead, lanes
        self.ssem, self.rsem = sems
        self.sbase, self.rbase = base
        self.subs = max(n for _, _, n in lanes)

    @staticmethod
    def counts(lanes):
        subs = max(n for _, _, n in lanes)
        return 1 + 3 * subs, 1 + 5 * subs

    def at(self, ln, changes):
        idx = list(self.pc.c)
        for d, v in changes:
            idx[d] = v
        return self.w.at[(*self.lead, *idx, ALL, ln)]

    def classes(self, i):
        return [k for k in CLASSES if i < self.lanes[k][2]]

    def stretch(self, k, i):
        lane0, width, subs = self.lanes[k]
        return pl.ds(lane0, width * subs) if i is None else pl.ds(lane0 + i * width, width)

    def wait(self, sem, n, i):
        lanes = sum(self.lanes[k][1] * (self.lanes[k][2] if i is None else 1) for k in self.classes(i or 0))
        box = [pl.ds(0, q) for q in n]
        ref = self.w.at[(*self.lead, *box, ALL, pl.ds(0, lanes))]
        arrived(ref, sem)

    def send(self, refs, ss, rs, d, v):
        for r in refs:
            remote(r, r, self.ssem.at[self.sbase + ss], self.rsem.at[self.rbase + rs], self.pc.dev(d, v)).start()

    def own_start(self):
        for k in CLASSES:
            d = ORDERS[k][0]
            for v in self.pc.others(d):
                self.send([self.at(self.stretch(k, None), ())], 0, 0, d, v)

    def own_end(self):
        self.wait(self.rsem.at[self.rbase], (3, 1, 1), None)

    def ring_start(self, i):
        for k in self.classes(i):
            d1, d, _ = ORDERS[k]
            for v in self.pc.others(d):
                self.send([self.at(self.stretch(k, i), ((d1, ALL),))], 1 + 3 * i, 1 + 5 * i, d, v)

    def ring_end(self, i):
        self.wait(self.rsem.at[self.rbase + 1 + 5 * i], (3, R, 1), i)

    def tree_refs(self, k, i, late, v, half):
        d1, d2, d3 = ORDERS[k]
        base = ((d1, part(half)), (d3, v))
        ln = self.stretch(k, i)
        return [self.at(ln, (*base, (d2, o))) for o in self.pc.others(d2)] if late else [self.at(ln, base)]

    def tree_start(self, i, late):
        for k in self.classes(i):
            d = ORDERS[k][2]
            for dirn in BOTH:
                refs = self.tree_refs(k, i, late, self.pc.c[d], None)
                self.send(refs, 2 + 3 * i + late, 2 + 5 * i + 2 * late, d, self.pc.near(d, dirn))

    def tree_mid(self, i, late):
        self.wait(self.rsem.at[self.rbase + 2 + 5 * i + 2 * late], (2, R, 3 if late else 1), i)
        for k in self.classes(i):
            d = ORDERS[k][2]
            for dirn in BOTH:
                refs = self.tree_refs(k, i, late, self.pc.near(d, 1 - dirn), dirn)
                self.send(refs, 2 + 3 * i + late, 3 + 5 * i + 2 * late, d, self.pc.near(d, dirn))

    def tree_end(self, i, late):
        self.wait(self.rsem.at[self.rbase + 3 + 5 * i + 2 * late], (1, R, 3 if late else 1), i)

    def drain(self):
        self.wait(self.ssem.at[self.sbase], (3, 1, 1), None)
        for i in range(self.subs):
            for q, n in enumerate(((3, R, 1), (3, R, 1), (3, R, 3))):
                self.wait(self.ssem.at[self.sbase + 1 + 3 * i + q], n, i)


class Scatter:
    def __init__(self, pc, pool, recv, sems, finish):
        self.pc, self.pool, self.recv, self.sems, self.finish = pc, pool, recv, sems, finish

    @staticmethod
    def place_of(u):
        v = u - U2
        return jnp.where(u < U2, 2 * U2 + u, R * lax.div(v, 2) + lax.rem(v, 2))

    def blk(self, u, k, ph, v, half):
        order = ORDERS[k]
        idx = [None] * len(order)
        for q in range(ph):
            idx[order[q]] = self.pc.c[order[q]]
        idx[order[ph]] = v
        free = [d for d in DIMS if idx[d] is None]
        for d in free:
            idx[d] = ALL
        lanes = ALL
        if free:
            idx[free[0]] = part(half)
        else:
            lanes = part(half, LANE)
        return self.pool.at[(self.place_of(u), *idx, ALL, lanes)]

    def landing(self, k, ph, slot, dirn, kind, half):
        r = self.recv[ph][kind].at[k, slot, dirn]
        if half is None or not kind:
            return r
        return r.at[part(half)] if ph < 2 else r.at[:, part(half, LANE)]

    def copy(self, n, k, ph, dirn, kind):
        d = ORDERS[k][ph]
        slot = lax.rem(n, SLOTS)
        near = self.pc.near(d, dirn)
        half = 1 - dirn if kind == 1 else dirn
        src = self.blk(n * 3 + k, k, ph, near if kind else self.pc.opp[d], half)
        dst = self.landing(k, ph, slot, dirn, min(kind, 1), half)
        return remote(src, dst, self.ssem(n, k // 2, ph), self.rsem(n, k // 2, ph, min(kind, 1)), self.pc.dev(d, near))

    def ssem(self, n, pair, ph):
        return self.sems[0].at[(ph * 2 + pair) * SLOTS + lax.rem(n, SLOTS)]

    def rsem(self, n, pair, ph, kind):
        return self.sems[1].at[((ph * 2 + pair) * 2 + kind) * SLOTS + lax.rem(n, SLOTS)]

    def received(self, n, pair, ph, kind):
        r, slot = self.recv[ph][kind], lax.rem(n, SLOTS)
        arrived(r.at[2, slot] if pair else r.at[pl.ds(0, 2), slot], self.rsem(n, pair, ph, kind))

    def sent(self, n, pair, ph):
        r = self.recv[ph][1]
        arrived(r.at[:, 0, 0] if pair else r.at[:, 0], self.ssem(n, pair, ph))

    def start(self, n, ks, ph):
        for kind in BOTH:
            for k in ks:
                for dirn in BOTH:
                    self.copy(n, k, ph, dirn, kind).start()

    def mid(self, n, ks, ph):
        self.received(n, ks[0] // 2, ph, 0)
        for k in ks:
            d = ORDERS[k][ph]
            for dirn in BOTH:
                b = self.blk(n * 3 + k, k, ph, self.pc.near(d, dirn), dirn)
                b[...] = b[...] + self.landing(k, ph, lax.rem(n, SLOTS), dirn, 0, None)[...]
        for k in ks:
            for dirn in BOTH:
                self.copy(n, k, ph, dirn, 2).start()

    def end(self, n, ks, ph):
        self.received(n, ks[0] // 2, ph, 1)
        for k in ks:
            own = self.blk(n * 3 + k, k, ph, self.pc.c[ORDERS[k][ph]], None)
            tot = own[...]
            for dirn in BOTH:
                tot = tot + self.landing(k, ph, lax.rem(n, SLOTS), dirn, 1, None)[...]
            if ph < 2:
                own[...] = tot
            else:
                self.finish(n * 3 + k, tot)
        self.sent(n, ks[0] // 2, ph)
        if ph < 2:
            self.start(n, ks, ph + 1)

    def each(self, n, fn):
        for ks in PAIRS:

            @pl.when((n >= 0) & (n < ROUNDS[ks[0]]))
            def _():
                fn(n, ks)

    def events(self, t):
        for ph in reversed(DIMS):
            self.each(t - 2 - 2 * ph, lambda n, ks: self.end(n, ks, ph))
            self.each(t - 1 - 2 * ph, lambda n, ks: self.mid(n, ks, ph))
        self.each(t, lambda n, ks: self.start(n, ks, 0))


def half_tanh(h, h2):
    return 0.5 * jnp.tanh(h * (C0 + C1 * h2))


def gelu(h):
    return h * (0.5 + half_tanh(h, h * h))


def gelu_slope(h):
    h2 = h * h
    t = half_tanh(h, h2)
    return (0.5 + t) + ((0.25 - t * t) * (2.0 * C0 + (6.0 * C1) * h2)) * h


def recv_shapes():
    out = []
    for ph in DIMS:
        lead, dims = (3, SLOTS, 2), [R] * (2 - ph)
        half = [2] + dims[1:] if dims else []
        out.append((*lead, *half, SUBL, COL if dims else LANE))
        out.append((*lead, *dims, SUBL, COL))
    return out


AG1, AG2 = Gather.counts(W1_LANES), Gather.counts(W2_LANES)
RS_SEMS = 3 * 2 * SLOTS
BLOCKS = DIM // COL


def kernel(xh, uph, dnh, gh, yo, gxo, dw1o, dw2o, landh, keeph, x, xt, g, w1, w2, a, pool, sb, dw1s, dw1l, *rest):
    recv, (ag_s, ag_r, rs_s, rs_r, lsem, xs, xr, spare_sem) = rest[:6], rest[6:]
    pc = Place()
    s = pc.s
    own, theirs = span(s, TOK), span(1 - s, TOK)
    my_lanes, their_lanes = span(s, HALF), span(1 - s, HALF)
    scope = jax.named_scope

    loads = [
        pltpu.make_async_copy(src, dst, lsem.at[i])
        for i, (src, dst) in enumerate((
            (uph.at[:, my_lanes], w1.at[(s, *pc.c)]),
            (dnh, w2.at[tuple(pc.c)]),
            (xh, x.at[own]),
            (gh, g.at[own]),
        ))
    ]
    for c in loads:
        c.start()

    with scope("bar"):
        bar = pltpu.get_barrier_semaphore()
        peers = [pc.partner] + [pc.dev(d, v) for d in DIMS for v in pc.others(d)]
        for dev in peers:
            pl.semaphore_signal(bar, inc=1, device_id=dev, device_id_type=MESH)
        pl.semaphore_wait(bar, len(peers))

    swaps = [
        remote(src, dst, xs.at[i], xr.at[i], pc.partner)
        for i, (src, dst) in enumerate((
            (uph.at[:, their_lanes], w1.at[(s, *pc.c)]),
            (xh, x.at[own]),
            (gh, g.at[own]),
        ))
    ]
    for c in swaps:
        c.start()

    g1 = Gather(pc, w1, (ALL,), W1_LANES, (ag_s, ag_r), (0, 0))
    g2 = Gather(pc, w2, (), W2_LANES, (ag_s, ag_r), AG1)

    w1f = w1.reshape(DIM, HALF)
    w2f = w2.reshape(HALF, DIM)
    units = pool.reshape(3 * U2, R * R * R, SUBL, COL)

    with scope("swapw"):
        loads[0].wait()
        swaps[0].wait_recv()
    g1.own_start()
    with scope("own"):
        g1.own_end()
    for i in range(3):
        g1.ring_start(i)
    for i in range(3):
        g1.tree_start(i, 0)
    loads[1].wait()
    g2.own_start()

    loads[2].wait()
    swaps[1].wait_recv()

    def turn(i, _):
        at = span(i, COL)
        xt[:, at] = x[at, :].T
        return 0

    with scope("turn"):
        lax.fori_loop(0, 2 * TOK // COL, turn, 0)

    def ring_done(i):
        with scope(f"ring{i}"):
            g1.ring_end(i)
        g1.tree_start(i, 1)

    ring_done(0)
    ring_done(1)
    with scope("early0"):
        g1.tree_mid(0, 0)
    with scope("late0"):
        g1.tree_mid(0, 1)
    with scope("early1"):
        g1.tree_mid(1, 0)
    ring_done(2)
    with scope("early2"):
        g1.tree_mid(2, 0)

    def rows(i):
        return slice(STEP * i, STEP * (i + 1))

    def flat(c, i):
        return units.at[R * c + i]

    def hidden_dot(c, i):
        sb[i % 2, :STEP] = dot(x[rows(i), :], w1f[:, span(c, COL)], NN)

    def hidden_act(c, i):
        h = sb[i % 2, :STEP]
        flat(c, i)[...] = h.reshape(STEP // SUBL, SUBL, COL)
        a[rows(i), span(c, COL)] = gelu(h).astype(bf16)

    def dhidden_dot(c, i):
        sb[i % 2, :STEP] = dot(g[rows(i), :], w2f[span(c, COL), :], NT)

    def dhidden_act(c, i):
        slope = gelu_slope(flat(c, i)[...].reshape(STEP, COL))
        a[rows(i), span(c, COL)] = (slope * sb[i % 2, :STEP]).astype(bf16)

    def grad1(c):
        r = dot(xt[...], a[:, span(c, COL)], NN)
        for p in BOTH:
            flat(c, p)[...] = r[rows(p)].reshape(STEP // SUBL, SUBL, COL)

    def chunk_steps(dot_step, act_step, c, after):
        for i in range(STEPS):
            if i + 1 < STEPS:
                dot_step(c, i + 1)
            else:
                dot_step(after, 0)
            act_step(c, i)

    def grad2(nb):
        def rows_of(c):
            r = dot(a[:, span(c, COL)], g[:, pl.ds(nb * 2 * COL, 2 * COL)], TN)
            for b in BOTH:
                rr = r[:, COL * b:COL * (b + 1)].reshape(SUBL, R, SUBL, COL)
                for q in range(R):
                    units[2 * U2 + R * (2 * nb + b) + q, span(c, SUBL)] = rr[:, q]

        def body(i, _):
            for q in range(R):
                rows_of(i * R + q)
            return 0

        lax.fori_loop(0, CHUNKS // R, body, 0)

    def product(at, nb, i):
        lanes = span(nb, COL)
        return dot(a[at, :], w1f[lanes, :], NT) if i else dot(a[at, :], w2f[:, lanes], NN)

    def out_block(nb, i):
        lanes = span(nb, COL)
        return pltpu.make_async_copy((x, g)[i].at[own, lanes], (yo, gxo)[i].at[:, lanes], lsem.at[R + BLOCKS * i + nb])

    def keep_y(n):
        return pltpu.make_async_copy(sb.at[lax.rem(n, 3)], keeph.at[n], lsem.at[12 + lax.rem(n, 3)])

    def give_y_block(nb):
        return remote(keeph.at[2 * nb], landh.at[nb], xs.at[3 + nb], xr.at[3 + nb], pc.partner)

    def kept(n):
        keep_y(n).wait()

        @pl.when(lax.rem(n, 2) == 0)
        def _():
            give_y_block(lax.div(n, 2)).start()

    def give_y(n):
        @pl.when(n > 2)
        def _():
            kept(n - 3)

        at = pl.ds(pl.multiple_of(TOK * jnp.where(lax.rem(n, 2) == 0, 1 - s, s), TOK), TOK)
        sb[lax.rem(n, 3)] = product(at, lax.div(n, 2), 0)
        keep_y(n).start()

    def finish_block(nb, i, at, part_sum):
        res, lanes = (x, g)[i], span(nb, COL)
        res[at, lanes] = (res[at, lanes].astype(f32) + part_sum).astype(bf16)

    def fetch_y(nb):
        return [pltpu.make_async_copy(src, sb.at[b], lsem.at[12 + b]) for b, src in enumerate((landh.at[nb], keeph.at[2 * nb + 1]))]

    def take_y(nb):
        give_y_block(nb).wait_recv()
        for c in fetch_y(nb):
            c.start()
        for c in fetch_y(nb):
            c.wait()

        def add(h, _):
            at = pl.ds(pl.multiple_of(TOK * s + COL * h, COL), COL)
            finish_block(nb, 0, at, sb[0, span(h, COL)] + sb[1, span(h, COL)])
            return 0

        lax.fori_loop(0, TOK // COL, add, 0)
        out_block(nb, 0).start()

    def spare(n):
        return units.at[pl.ds(R * n + 2, 2)]

    def give_gx_block(nb):
        return remote(spare(BLOCKS + nb), spare(nb), xs.at[3 + BLOCKS + nb], xr.at[3 + BLOCKS + nb], pc.partner)

    def give_gx(nb):
        spare(BLOCKS + nb)[...] = product(theirs, nb, 1).reshape(2, TOK // 2 // SUBL, SUBL, COL)
        give_gx_block(nb).start()

    def take_gx(nb):
        give_gx_block(nb).wait_recv()

        def add(h, _):
            at = pl.ds(pl.multiple_of(TOK * s + STEP * h, STEP), STEP)
            finish_block(nb, 1, at, product(at, nb, 1) + flat(nb, 2 + h)[...].reshape(STEP, COL))
            return 0

        lax.fori_loop(0, TOK // STEP, add, 0)
        out_block(nb, 1).start()

    def loop(n, fn):
        def body(i, _):
            fn(i)
            return 0

        lax.fori_loop(0, n, body, 0)

    def at(t, first, fn, last=None):
        @pl.when((t >= first) & (t <= (first if last is None else last)))
        def _():
            with scope(f"task{first}"):
                fn()

    def arrive(i):
        g1.tree_end(i, 0)
        g1.tree_end(i, 1)

    def w2_ring():
        g2.own_end()
        g2.ring_start(0)
        g2.tree_start(0, 0)

    def w2_late():
        g2.ring_end(0)
        g2.tree_start(0, 1)
        g2.tree_mid(0, 0)

    def chunk(q):
        return lax.div(q, 3) + 3 * lax.rem(q, 3)

    with scope("arrive"):
        arrive(0)
    hidden_dot(0, 0)

    def hidden_step(q):
        at(q, 0, lambda: g1.tree_mid(1, 1))
        at(q, 1, lambda: g1.tree_mid(2, 1))
        at(q, 1, w2_ring)
        at(q, 2, lambda: arrive(1))
        at(q, 5, lambda: arrive(2))
        at(q, 5, w2_late)
        with scope("hidden"):
            chunk_steps(hidden_dot, hidden_act, chunk(q), chunk(jnp.minimum(q + 1, CHUNKS - 1)))

    loop(CHUNKS, hidden_step)
    loads[3].wait()
    swaps[2].wait_recv()
    with scope("gradtwo"):
        grad2(0)
    with scope("w2mid"):
        g2.tree_mid(0, 1)

    def finish(u, tot):
        @pl.when(u < U2)
        def _():
            dw2o[span(lax.rem(u, R), SUBL), span(lax.div(u, R), COL)] = tot

        @pl.when(u >= U2)
        def _():
            v = u - U2
            dw1s[lax.rem(v, 2), :, span(lax.div(v, 2), COL)] = tot

    rs = Scatter(pc, pool, [recv[2 * ph:2 * ph + 2] for ph in DIMS], (rs_s, rs_r), finish)

    def slot(t, _):
        with scope("ev"):
            rs.events(t)

        def first_task():
            grad2(1)
            for i in BOTH:
                g2.tree_end(0, i)
            g1.drain()
            g2.drain()

        at(t, 0, first_task)
        at(t, 1, lambda: loop(BLOCKS, lambda i: give_y(BLOCKS * (t - 1) + i)), 2)

        def first_dot():
            for n in range(3):
                kept(2 * BLOCKS - 3 + n)
            dhidden_dot(0, 0)

        def dhidden(c):
            chunk_steps(dhidden_dot, dhidden_act, c, jnp.minimum(c + 1, CHUNKS - 1))
            grad1(c)

        at(t, 3, first_dot)
        at(t, 3, lambda: loop(2, lambda i: dhidden(2 * (t - 3) + i)), 6)
        at(t, 5, lambda: pl.semaphore_signal(spare_sem, inc=1, device_id=pc.partner, device_id_type=MESH))
        at(t, 7, lambda: pl.semaphore_wait(spare_sem, 1))
        at(t, 7, lambda: loop(BLOCKS, give_gx))
        at(t, 8, lambda: loop(2, lambda i: take_y(2 * (t - 8) + i)), 9)
        at(t, 10, lambda: loop(2, lambda i: take_gx(2 * (t - 10) + i)), 11)
        return 0

    lax.fori_loop(0, max(ROUNDS) + 6, slot, 0)

    with scope("last"):
        last = remote(dw1s.at[1 - s], dw1l, xs.at[11], xr.at[11], pc.partner)
        last.start()
        dw1o[:, my_lanes] = dw1s[s]
        for c in swaps:
            c.wait_send()
        for nb in range(BLOCKS):
            give_y_block(nb).wait_send()
            give_gx_block(nb).wait_send()
        for i in BOTH:
            for nb in range(BLOCKS):
                out_block(nb, i).wait()
        last.wait()
        dw1o[:, their_lanes] = dw1l[...]


def local_stack(x, up, down, g):
    shape = jax.ShapeDtypeStruct
    dma = pltpu.SemaphoreType.DMA
    bf = [(2 * TOK, DIM), (DIM, 2 * TOK), (2 * TOK, DIM), (2, R, R, R, SUBL, HALF), (R, R, R, HALF // R**3, DIM), (2 * TOK, HALF)]
    ff = [(3 * U2, R, R, R, SUBL, COL), (3, TOK, COL), (2, SUBL, HALF), (SUBL, HALF)] + recv_shapes()
    call = pl.pallas_call(
        kernel,
        out_shape=(
            shape(x.shape, bf16),
            shape(g.shape, bf16),
            shape(up.shape[1:], f32),
            shape(down.shape[1:], f32),
            shape((BLOCKS, TOK, COL), f32),
            shape((2 * BLOCKS, TOK, COL), f32),
        ),
        in_specs=[ANY] * 4,
        out_specs=(ANY, ANY, VMEM, VMEM, ANY, ANY),
        scratch_shapes=[pltpu.VMEM(q, bf16) for q in bf] + [pltpu.VMEM(q, f32) for q in ff]
        + [dma((n,)) for n in (AG1[0] + AG2[0], AG1[1] + AG2[1], RS_SEMS, 2 * RS_SEMS, 15, 12, 12)] + [pltpu.SemaphoreType.REGULAR],
        compiler_params=pltpu.CompilerParams(collective_id=0, has_side_effects=True, vmem_limit_bytes=67043328),
        name="stack",
    )
    y, gx, dw1, dw2 = call(x, up[0], down[0], g)[:4]
    return y, gx, dw1[None], dw2[None]


def solution(mesh):
    tok, mat = P(AXES, None), P(None, AXES, None)
    return jax.shard_map(local_stack, mesh=mesh, in_specs=(tok, mat, mat, tok), out_specs=(tok, tok, mat, mat), check_vma=False)
```

time: 1600 us -> 149 us (0.09)
  waiting for transfers between devices: 1460 us -> 0 us
  Pallas kernels: 0 us -> 142 us
  matrix products: 105 us -> 0 us
    reduce_scatter x1 -> x0, waiting for transfers between devices: 688 us -> none  [local_stack(): lax.psum_scatter(down_part, SHARD_AXES, scatter_dimension=0, tiled=True)]
    unnamed x5 -> x0, waiting for transfers between devices: 639 us -> none
    pallas_call x0 -> x1, Pallas kernels: none -> 142 us  [local_stack(): y, gx, dw1, dw2 = call(x, up[0], down[0], g)[:4]]
    all_gather x2 -> x0, waiting for transfers between devices: 130 us -> none  [the longest x1 75.6 us: local_stack(): up_full = lax.all_gather(up_loc[layer_idx], SHARD_AXES, axis=0, tiled=True)]
    dot_general x6 -> x0, matrix products: 105 us -> none  [the longest x1 22.8 us: local_stack(): lax.dot_general(grad_now, down_full, CONTRACT_LAST, preferred_element_typ...]
  transfers between devices with their start and end apart: 4 -> 0, of which waited for: 4 -> 0; matrix products, arithmetic and copies ran while one was open for 4% -> 0% of each run, Pallas kernels for 0% -> 0%
where the time goes in v1:
time: 149 us; the launch traced here: 148 us
  Pallas kernels  142 us (95%)
  local copies, waits for them, and re-layouts  5.87 us (4%)
    pallas_call x1, Pallas kernels, local_stack(): y, gx, dw1, dw2 = call(x, up[0], down[0], g)[:4]  142 us
    unnamed x10, local copies, waits for them, and re-layouts  5.87 us

profile of v1, /device:TPU:1, one launch (start us, length us, event | category | flops | bytes accessed | tf_op | source)
XLA Modules:
  0.0 148.5 jit_solution(14924649329418628141)
XLA Ops:
  0.6 142.0 %stack.1 = (bf16[1024,1024]{1,0:T(8,128)(2,1)}, bf16[1024,1024]{1,0:T(8,128)(2,1)}, f32[8,4096]{1,0:T(8,128)}, f32[32,1024]{1,0:T(8,128)}, f32[4,1024,256]{2,1,0:T(8,128)}, /*index=5*/f32[8,1024,256]{2,1,0:T(8,128)}) custom-call(bf16[1024,1024]{1,0:T(8,128)(2,1)} %xh.1, bf16[8,4096]{1,0:T(8,128)(2,1)} %bitcast.6, bf16[32,1024]{1,0:T(8,128)(2,1)} %bitcast.7, ...), custom_call_target="tpu_custom_call" | custom-call | tf_op jit(solution)/shard_map/stack/pallas_call | solution.py:634
  142.6 0.0 copy-start
  142.6 3.2 %copy.12 = bf16[1024,1024]{1,0:T(8,128)(2,1)} copy(bf16[1024,1024]{1,0:T(8,128)(2,1)} %get-tuple-element.16) | data formatting | bytes 4194304
  145.8 0.0 copy-done
  145.8 0.0 copy-start.2
  145.9 0.0 copy-start.1
  145.9 1.3 copy.13
  147.2 0.0 copy-done.2
  147.2 0.7 copy.14
  147.8 0.0 copy-done.1
  147.8 0.7 copy.15
Async XLA Ops:
  142.6 3.2 %copy-start = (bf16[1024,1024]{1,0:T(8,128)(2,1)S(1)}, bf16[1024,1024]{1,0:T(8,128)(2,1)}, u32[]{:S(2)}) copy-start(bf16[1024,1024]{1,0:T(8,128)(2,1)} %get-tuple-element.17) | copy-start | bytes 6291460
  145.8 1.3 copy-start.2
  145.9 2.0 %copy-start.1 = (f32[32,1024]{1,0:T(8,128)S(1)}, f32[32,1024]{1,0:T(8,128)}, u32[]{:S(2)}) copy-start(f32[32,1024]{1,0:T(8,128)} %get-tuple-element.11) | copy-start | bytes 393220

commit v2 on v1

v2 whole, which is shorter than its diff:
```python
import jax
import jax.numpy as jnp
from jax import lax
from jax.experimental import pallas as pl
from jax.experimental.pallas import tpu as pltpu
from jax.sharding import PartitionSpec as P

f32, bf16 = jnp.float32, jnp.bfloat16
MESH = pl.DeviceIdType.MESH
NN, NT, TN = [(((i,), (k,)), ((), ())) for i, k in ((1, 0), (1, 1), (0, 0))]
ANY = pl.BlockSpec(memory_space=pl.ANY)
VMEM = pl.BlockSpec(memory_space=pltpu.VMEM)
AXES = ("sub", "fsdp")

TOK = 1024
DIM = 1024
HALF = 2048
R = 4
SUBL = 8
COL = 256
CHUNKS = HALF // COL
STEP = 512
STEPS = 2 * TOK // STEP
U2 = 16
SLOTS = 4
ROUNDS = (11, 11, 10)
CLASSES = DIMS = range(3)
PAIRS = ((0, 1), (2,))
BOTH = range(2)
ORDERS = ((0, 1, 2), (1, 2, 0), (2, 0, 1))
STRIDE = (R * R, R, 1)
C0 = 0.7978845608028654
C1 = 0.044715 * C0
ALL = slice(None)

W1_LANES = ((0, COL, 3), (3 * COL, COL, 3), (6 * COL, COL, 2))
W2_LANES = ((0, 256, 1), (256, 384, 1), (640, 384, 1))


def dot(a, b, dims):
    return lax.dot_general(a, b, dims, preferred_element_type=f32)


def span(i, n):
    return pl.ds(pl.multiple_of(i * n, n), n)


class Place:
    def __init__(self):
        self.s, self.j = lax.axis_index("sub"), lax.axis_index("fsdp")
        self.c = [lax.rem(lax.div(self.j, n), R) for n in STRIDE]
        self.plus, self.minus, self.opp = [[lax.rem(c + o, R) for c in self.c] for o in (1, 3, 2)]
        self.partner = (1 - self.s, self.j)

    def dev(self, d, v):
        return (self.s, self.j + (v - self.c[d]) * STRIDE[d])

    def near(self, d, dirn):
        return self.minus[d] if dirn else self.plus[d]

    def others(self, d):
        return self.plus[d], self.minus[d], self.opp[d]


def remote(src, dst, ssem, rsem, dev):
    return pltpu.make_async_remote_copy(src, dst, ssem, rsem, device_id=dev, device_id_type=MESH)


def arrived(ref, sem):
    pltpu.make_async_copy(ref, ref, sem).wait()


def part(half):
    return ALL if half is None else pl.ds(2 * half, 2)


class Gather:
    def __init__(self, pc, w, lead, lanes, sems, base):
        self.pc, self.w, self.lead, self.lanes, self.sems, self.base = pc, w, lead, lanes, sems, base

    @staticmethod
    def count(lanes):
        return 1 + 3 * max(n for _, _, n in lanes)

    def at(self, ln, changes):
        idx = list(self.pc.c)
        for d, v in changes:
            idx[d] = v
        return self.w.at[(*self.lead, *idx, ALL, ln)]

    def classes(self, i):
        return [k for k in CLASSES if i < self.lanes[k][2]]

    def stretch(self, k, step, i):
        lane0, width, subs = self.lanes[k]
        return pl.ds(lane0 + i * width, width) if step else pl.ds(lane0, width * subs)

    def sem(self, q, step, i):
        return self.sems[q].at[self.base + (3 * i + step if step else 0)]

    def send(self, block, step, halves, i, d, v):
        remote(block, block, self.sem(0, step, i), self.sem(1, step + halves, i), self.pc.dev(d, v)).start()

    def start(self, step, i=0):
        for k in self.classes(i):
            block = self.at(self.stretch(k, step, i), [(d, ALL) for d in ORDERS[k][:step]])
            d = ORDERS[k][step]
            for v in self.pc.others(d)[:3 if step < 2 else 2]:
                self.send(block, step, 0, i, d, v)

    def mid(self, i=0):
        self.wait(1, 2, 0, i, 2)
        for k in self.classes(i):
            d1, d2, d = ORDERS[k]
            for dirn in BOTH:
                behind = self.pc.near(d, 1 - dirn)
                block = self.at(self.stretch(k, 2, i), ((d1, part(dirn)), (d2, ALL), (d, behind)))
                self.send(block, 2, 1, i, d, self.pc.near(d, dirn))

    def wait(self, q, step, halves, i, n):
        lanes = sum(self.lanes[k][1] * (1 if step else self.lanes[k][2]) for k in self.classes(i))
        box = [pl.ds(0, m) for m in (n, *[R] * step, *[1] * (2 - step))]
        arrived(self.w.at[(*self.lead, *box, ALL, pl.ds(0, lanes))], self.sem(q, step + halves, i))

    def end(self, step, i=0):
        if step < 2:
            self.wait(1, step, 0, i, 3)
        else:
            self.wait(1, step, 1, i, 1)

    def drain(self):
        self.wait(0, 0, 0, 0, 3)
        for i in range(max(n for _, _, n in self.lanes)):
            for step in (1, 2):
                self.wait(0, step, 0, i, 3)


class Scatter:
    def __init__(self, pc, pool, recv, sems, finish):
        self.pc, self.pool, self.recv, self.sems, self.finish = pc, pool, recv, sems, finish

    @staticmethod
    def place_of(u):
        v = u - U2
        return jnp.where(u < U2, 2 * U2 + u, R * lax.div(v, 2) + lax.rem(v, 2))

    def blk(self, u, k, ph, v, half):
        order = ORDERS[k]
        idx = [None] * len(order)
        for q in range(ph):
            idx[order[q]] = self.pc.c[order[q]]
        idx[order[ph]] = v
        free = [d for d in DIMS if idx[d] is None]
        for d in free:
            idx[d] = ALL
        if free:
            idx[free[0]] = part(half)
        return self.pool.at[(self.place_of(u), *idx)]

    def landing(self, k, ph, slot, dirn, kind, half):
        r = self.recv[ph][kind].at[k, slot, dirn]
        return r if half is None or not kind else r.at[part(half)]

    def ssem(self, n, pair, ph):
        return self.sems[0].at[(ph * 2 + pair) * SLOTS + lax.rem(n, SLOTS)]

    def rsem(self, n, pair, ph, kind):
        return self.sems[1].at[((ph * 2 + pair) * 2 + kind) * SLOTS + lax.rem(n, SLOTS)]

    def send(self, n, k, ph, src, dst, kind, v):
        pair = k // 2
        remote(src, dst, self.ssem(n, pair, ph), self.rsem(n, pair, ph, kind), self.pc.dev(ORDERS[k][ph], v)).start()

    def copy(self, n, k, ph, dirn, kind):
        d = ORDERS[k][ph]
        near = self.pc.near(d, dirn)
        half = 1 - dirn if kind == 1 else dirn
        src = self.blk(n * 3 + k, k, ph, near if kind else self.pc.opp[d], half)
        dst = self.landing(k, ph, lax.rem(n, SLOTS), dirn, min(kind, 1), half)
        self.send(n, k, ph, src, dst, min(kind, 1), near)

    def received(self, n, pair, ph, kind):
        r, slot = self.recv[ph][kind], lax.rem(n, SLOTS)
        arrived(r.at[2, slot] if pair else r.at[pl.ds(0, 2), slot], self.rsem(n, pair, ph, kind))

    def sent(self, n, pair, ph):
        r = self.recv[ph][1]
        if ph < 2:
            ref = r.at[:, 0, 0] if pair else r.at[:, 0]
        else:
            ref = r.at[2, 0] if pair else r.at[pl.ds(0, 2), 0]
        arrived(ref, self.ssem(n, pair, ph))

    def start(self, n, ks, ph):
        for kind in BOTH:
            for k in ks:
                for dirn in BOTH:
                    self.copy(n, k, ph, dirn, kind)

    def start_last(self, n, ks):
        for k in ks:
            for i, v in enumerate(self.pc.others(ORDERS[k][2])):
                self.send(n, k, 2, self.blk(n * 3 + k, k, 2, v, None), self.recv[2][1].at[k, lax.rem(n, SLOTS), i], 1, v)

    def mid(self, n, ks, ph):
        self.received(n, ks[0] // 2, ph, 0)
        for k in ks:
            d = ORDERS[k][ph]
            for dirn in BOTH:
                b = self.blk(n * 3 + k, k, ph, self.pc.near(d, dirn), dirn)
                b[...] = b[...] + self.landing(k, ph, lax.rem(n, SLOTS), dirn, 0, None)[...]
        for k in ks:
            for dirn in BOTH:
                self.copy(n, k, ph, dirn, 2)

    def end(self, n, ks, ph):
        self.received(n, ks[0] // 2, ph, 1)
        for k in ks:
            own = self.blk(n * 3 + k, k, ph, self.pc.c[ORDERS[k][ph]], None)
            tot = own[...]
            for i in range(3 if ph == 2 else 2):
                tot = tot + self.recv[ph][1].at[k, lax.rem(n, SLOTS), i][...]
            if ph < 2:
                own[...] = tot
            else:
                self.finish(n * 3 + k, tot)
        self.sent(n, ks[0] // 2, ph)
        if ph == 0:
            self.start(n, ks, 1)
        elif ph == 1:
            self.start_last(n, ks)

    def each(self, n, fn):
        for ks in PAIRS:

            @pl.when((n >= 0) & (n < ROUNDS[ks[0]]))
            def _():
                fn(n, ks)

    def events(self, t):
        self.each(t - 5, lambda n, ks: self.end(n, ks, 2))
        for ph in (1, 0):
            self.each(t - 2 - 2 * ph, lambda n, ks: self.end(n, ks, ph))
            self.each(t - 1 - 2 * ph, lambda n, ks: self.mid(n, ks, ph))
        self.begin(t + 1)

    def begin(self, n):
        self.each(n, lambda n, ks: self.start(n, ks, 0))


def half_tanh(h, h2):
    return 0.5 * jnp.tanh(h * (C0 + C1 * h2))


def gelu(h):
    return h * (0.5 + half_tanh(h, h * h))


def gelu_slope(h):
    h2 = h * h
    t = half_tanh(h, h2)
    return (0.5 + t) + ((0.25 - t * t) * (2.0 * C0 + (6.0 * C1) * h2)) * h


def recv_shapes():
    out = []
    for dims in ((R, R), (R,)):
        for q in ((2, *dims[1:]), dims):
            out.append((3, SLOTS, 2, *q, SUBL, COL))
    return out + [(3, SLOTS, 3, SUBL, COL)]


AG1, AG2 = Gather.count(W1_LANES), Gather.count(W2_LANES)
RS_SEMS = 3 * 2 * SLOTS
BLOCKS = DIM // COL


def kernel(xh, uph, dnh, gh, yo, gxo, dw1o, dw2o, landh, keeph, x, xt, g, w1, w2, a, pool, sb, dw1s, dw1l, *rest):
    recv, (ag_s, ag_r, rs_s, rs_r, lsem, xs, xr, spare_sem) = rest[:5], rest[5:]
    pc = Place()
    s = pc.s
    own, theirs = span(s, TOK), span(1 - s, TOK)
    my_lanes, their_lanes = span(s, HALF), span(1 - s, HALF)
    scope = jax.named_scope

    loads = [
        pltpu.make_async_copy(src, dst, lsem.at[i])
        for i, (src, dst) in enumerate((
            (uph.at[:, my_lanes], w1.at[(s, *pc.c)]),
            (dnh, w2.at[tuple(pc.c)]),
            (xh, x.at[own]),
            (gh, g.at[own]),
        ))
    ]
    for c in loads:
        c.start()

    with scope("bar"):
        bar = pltpu.get_barrier_semaphore()
        peers = [pc.partner] + [pc.dev(d, v) for d in DIMS for v in pc.others(d)]
        for dev in peers:
            pl.semaphore_signal(bar, inc=1, device_id=dev, device_id_type=MESH)
        pl.semaphore_wait(bar, len(peers))

    swaps = [
        remote(src, dst, xs.at[i], xr.at[i], pc.partner)
        for i, (src, dst) in enumerate((
            (uph.at[:, their_lanes], w1.at[(s, *pc.c)]),
            (xh, x.at[own]),
            (gh, g.at[own]),
        ))
    ]
    for c in swaps:
        c.start()

    g1 = Gather(pc, w1, (ALL,), W1_LANES, (ag_s, ag_r), 0)
    g2 = Gather(pc, w2, (), W2_LANES, (ag_s, ag_r), AG1)

    w1f = w1.reshape(DIM, HALF)
    w2f = w2.reshape(HALF, DIM)
    units = pool.reshape(3 * U2, R * R * R, SUBL, COL)

    with scope("swapw"):
        loads[0].wait()
        swaps[0].wait_recv()
    g1.start(0)
    loads[1].wait()
    g2.start(0)
    with scope("own"):
        g1.end(0)
    for i in range(3):
        g1.start(1, i)
    with scope("own2"):
        g2.end(0)
    g2.start(1)
    for i in BOTH:
        with scope("ring"):
            g1.end(1, i)
        g1.start(2, i)
    with scope("mid"):
        g1.mid(0)
    with scope("ring"):
        g1.end(1, 2)
    g1.start(2, 2)
    with scope("mid"):
        g1.mid(1)
    with scope("ring2"):
        g2.end(1)
    g2.start(2)

    def turn(i, _):
        at = span(i, COL)
        xt[:, at] = x[at, :].T
        return 0

    loads[2].wait()
    swaps[1].wait_recv()
    with scope("turn"):
        lax.fori_loop(0, 2 * TOK // COL, turn, 0)

    def rows(i):
        return slice(STEP * i, STEP * (i + 1))

    def flat(c, i):
        return units.at[R * c + i]

    def hidden_dot(c, i):
        sb[i % 2, :STEP] = dot(x[rows(i), :], w1f[:, span(c, COL)], NN)

    def hidden_act(c, i):
        h = sb[i % 2, :STEP]
        flat(c, i)[...] = h.reshape(STEP // SUBL, SUBL, COL)
        a[rows(i), span(c, COL)] = gelu(h).astype(bf16)

    def dhidden_dot(c, i):
        sb[i % 2, :STEP] = dot(g[rows(i), :], w2f[span(c, COL), :], NT)

    def dhidden_act(c, i):
        slope = gelu_slope(flat(c, i)[...].reshape(STEP, COL))
        a[rows(i), span(c, COL)] = (slope * sb[i % 2, :STEP]).astype(bf16)

    def grad1(c):
        r = dot(xt[...], a[:, span(c, COL)], NN)
        for p in BOTH:
            flat(c, p)[...] = r[rows(p)].reshape(STEP // SUBL, SUBL, COL)

    def chunk_steps(dot_step, act_step, c, after):
        for i in range(STEPS):
            if i + 1 < STEPS:
                dot_step(c, i + 1)
            else:
                dot_step(after, 0)
            act_step(c, i)

    def grad2_rows(c, nb):
        r = dot(a[:, span(c, COL)], g[:, pl.ds(nb * 2 * COL, 2 * COL)], TN)
        for b in BOTH:
            rr = r[:, COL * b:COL * (b + 1)].reshape(SUBL, R, SUBL, COL)
            for q in range(R):
                units[2 * U2 + R * (2 * nb + b) + q, span(c, SUBL)] = rr[:, q]

    def grad2(nb):
        def body(i, _):
            for q in range(R):
                grad2_rows(i * R + q, nb)
            return 0

        lax.fori_loop(0, CHUNKS // R, body, 0)

    def product(at, nb, i):
        lanes = span(nb, COL)
        return dot(a[at, :], w1f[lanes, :], NT) if i else dot(a[at, :], w2f[:, lanes], NN)

    def out_block(nb, i):
        lanes = span(nb, COL)
        return pltpu.make_async_copy((x, g)[i].at[own, lanes], (yo, gxo)[i].at[:, lanes], lsem.at[R + BLOCKS * i + nb])

    def keep_y(n):
        return pltpu.make_async_copy(sb.at[lax.rem(n, 3)], keeph.at[n], lsem.at[12 + lax.rem(n, 3)])

    def give_y_block(nb):
        return remote(keeph.at[2 * nb], landh.at[nb], xs.at[3 + nb], xr.at[3 + nb], pc.partner)

    def kept(n):
        keep_y(n).wait()

        @pl.when(lax.rem(n, 2) == 0)
        def _():
            give_y_block(lax.div(n, 2)).start()

    def give_y(n):
        @pl.when(n > 2)
        def _():
            kept(n - 3)

        at = pl.ds(pl.multiple_of(TOK * jnp.where(lax.rem(n, 2) == 0, 1 - s, s), TOK), TOK)
        sb[lax.rem(n, 3)] = product(at, lax.div(n, 2), 0)
        keep_y(n).start()

    def finish_block(nb, i, at, part_sum):
        res, lanes = (x, g)[i], span(nb, COL)
        res[at, lanes] = (res[at, lanes].astype(f32) + part_sum).astype(bf16)

    def fetched_y(nb):
        return [pltpu.make_async_copy(src, sb.at[b], lsem.at[12 + b]) for b, src in enumerate((landh.at[nb], keeph.at[2 * nb + 1]))]

    def fetch_y(nb):
        give_y_block(nb).wait_recv()
        for c in fetched_y(nb):
            c.start()

    def take_y(nb):
        for c in fetched_y(nb):
            c.wait()

        def add(h, _):
            at = pl.ds(pl.multiple_of(TOK * s + COL * h, COL), COL)
            finish_block(nb, 0, at, sb[0, span(h, COL)] + sb[1, span(h, COL)])
            return 0

        lax.fori_loop(0, TOK // COL, add, 0)
        out_block(nb, 0).start()

    def spare(n):
        return units.at[pl.ds(R * n + 2, 2)]

    def give_gx_block(nb):
        return remote(spare(BLOCKS + nb), spare(nb), xs.at[3 + BLOCKS + nb], xr.at[3 + BLOCKS + nb], pc.partner)

    def give_gx(nb):
        spare(BLOCKS + nb)[...] = product(theirs, nb, 1).reshape(2, TOK // 2 // SUBL, SUBL, COL)
        give_gx_block(nb).start()

    def take_gx(nb):
        give_gx_block(nb).wait_recv()

        def add(h, _):
            at = pl.ds(pl.multiple_of(TOK * s + STEP * h, STEP), STEP)
            finish_block(nb, 1, at, product(at, nb, 1) + flat(nb, 2 + h)[...].reshape(STEP, COL))
            return 0

        lax.fori_loop(0, TOK // STEP, add, 0)
        out_block(nb, 1).start()

    def loop(n, fn):
        def body(i, _):
            fn(i)
            return 0

        lax.fori_loop(0, n, body, 0)

    def at(t, first, fn, last=None):
        @pl.when((t >= first) & (t <= (first if last is None else last)))
        def _():
            with scope(f"task{first}"):
                fn()

    def columns(i, _):
        with scope("arrive"):
            for q in range(3):
                at(i, q, lambda q=q: g1.end(2, q))
        at(i, 2, g2.mid)
        n = jnp.where(i < 2, 3, 2)
        hidden_dot(i, 0)

        def step(q, _):
            at(3 * i + q, 2, lambda: g1.mid(2))
            chunk_steps(hidden_dot, hidden_act, i + 3 * q, i + 3 * jnp.minimum(q + 1, n - 1))
            return 0

        with scope("hidden"):
            lax.fori_loop(0, n, step, 0)
        with scope("gradtwo"):
            for last in (1, 2):

                @pl.when((i < 2) if last == 2 else (i == 2))
                def _():
                    for q in range(last + 1):
                        grad2_rows(i + 3 * q, 0)

        return 0

    loads[3].wait()
    swaps[2].wait_recv()
    lax.fori_loop(0, 3, columns, 0)

    def finish(u, tot):
        @pl.when(u < U2)
        def _():
            dw2o[span(lax.rem(u, R), SUBL), span(lax.div(u, R), COL)] = tot

        @pl.when(u >= U2)
        def _():
            v = u - U2
            dw1s[lax.rem(v, 2), :, span(lax.div(v, 2), COL)] = tot

    rs = Scatter(pc, pool, [recv[:2], recv[2:4], (None, recv[4])], (rs_s, rs_r), finish)

    def first_dot():
        for n in range(3):
            kept(2 * BLOCKS - 3 + n)
        dhidden_dot(0, 0)

    def dhidden(c):
        chunk_steps(dhidden_dot, dhidden_act, c, jnp.minimum(c + 1, CHUNKS - 1))
        grad1(c)

    def settle():
        g2.end(2)
        g1.drain()
        g2.drain()

    def chunks_before(t):
        return jnp.clip(2 * (t - 3), 0, CHUNKS)

    with scope("start"):
        rs.begin(jnp.int32(0))

    def slot(t, _):
        with scope("ev"):
            rs.events(t)

        at(t, 0, lambda: grad2(1))
        at(t, 0, settle)
        at(t, 1, lambda: loop(BLOCKS, lambda i: give_y(BLOCKS * (t - 1) + i)), 2)
        at(t, 3, first_dot)

        def more(c, _):
            with scope("dh"):
                dhidden(c)
            return 0

        lax.fori_loop(chunks_before(t), chunks_before(t + 1), more, 0)
        at(t, 5, lambda: pl.semaphore_signal(spare_sem, inc=1, device_id=pc.partner, device_id_type=MESH))
        at(t, 7, lambda: pl.semaphore_wait(spare_sem, 1))

        def tokens(nb):
            fetch_y(nb)
            give_gx(nb)
            take_y(nb)

        at(t, 7, lambda: loop(2, lambda i: tokens(2 * (t - 7) + i)), 8)
        at(t, 9, lambda: take_gx(t - 9), 12)
        return 0

    lax.fori_loop(0, max(ROUNDS) + 5, slot, 0)

    with scope("last"):
        last = remote(dw1s.at[1 - s], dw1l, xs.at[11], xr.at[11], pc.partner)
        last.start()
        dw1o[:, my_lanes] = dw1s[s]
        for c in swaps:
            c.wait_send()
        for nb in range(BLOCKS):
            give_y_block(nb).wait_send()
            give_gx_block(nb).wait_send()
        for i in BOTH:
            for nb in range(BLOCKS):
                out_block(nb, i).wait()
        last.wait()
        dw1o[:, their_lanes] = dw1l[...]


def copy_out(*refs):
    n = (len(refs) - 2) // 3
    src, dst, mid, (into, out) = refs[:n], refs[n:2 * n], refs[2 * n:3 * n], refs[3 * n:]
    pieces = []
    for refs_of in zip(src, mid, dst):
        rows = max(refs_of[0].shape[0] // 2, SUBL)
        pieces += [[q.at[pl.ds(h, rows)] for q in refs_of] for h in range(0, refs_of[0].shape[0], rows)]
    steps = [[pltpu.make_async_copy(p[e], p[e + 1], sem.at[i]) for e, sem in enumerate((into, out))] for i, p in enumerate(pieces)]
    for first, _ in steps:
        first.start()
    for first, second in steps:
        first.wait()
        second.start()
    for _, second in steps:
        second.wait()


def local_stack(x, up, down, g):
    shape = jax.ShapeDtypeStruct
    dma = pltpu.SemaphoreType.DMA
    bf = [(2 * TOK, DIM), (DIM, 2 * TOK), (2 * TOK, DIM), (2, R, R, R, SUBL, HALF), (R, R, R, HALF // R**3, DIM), (2 * TOK, HALF)]
    ff = [(3 * U2, R, R, R, SUBL, COL), (3, TOK, COL), (2, SUBL, HALF), (SUBL, HALF)] + recv_shapes()
    call = pl.pallas_call(
        kernel,
        out_shape=(
            shape(x.shape, bf16),
            shape(g.shape, bf16),
            shape(up.shape[1:], f32),
            shape(down.shape[1:], f32),
            shape((BLOCKS, TOK, COL), f32),
            shape((2 * BLOCKS, TOK, COL), f32),
        ),
        in_specs=[ANY] * 4,
        out_specs=(ANY, ANY, VMEM, VMEM, ANY, ANY),
        scratch_shapes=[pltpu.VMEM(q, bf16) for q in bf] + [pltpu.VMEM(q, f32) for q in ff]
        + [dma((n,)) for n in (AG1 + AG2, AG1 + AG2, RS_SEMS, 2 * RS_SEMS, 15, 12, 12)] + [pltpu.SemaphoreType.REGULAR],
        compiler_params=pltpu.CompilerParams(collective_id=0, has_side_effects=True, vmem_limit_bytes=67043328),
        name="stack",
    )
    res = call(x, up[0], down[0], g)[:4]
    y, gx, dw1, dw2 = pl.pallas_call(
        copy_out,
        out_shape=[shape(q.shape, q.dtype) for q in res],
        in_specs=[ANY] * 4,
        out_specs=[ANY] * 4,
        scratch_shapes=[pltpu.VMEM(q.shape, q.dtype) for q in res] + [dma((2 * 4,))] * 2,
        name="copy_out",
    )(*res)
    return y, gx, dw1[None], dw2[None]


def solution(mesh):
    tok, mat = P(AXES, None), P(None, AXES, None)
    return jax.shard_map(local_stack, mesh=mesh, in_specs=(tok, mat, mat, tok), out_specs=(tok, tok, mat, mat), check_vma=False)
```

time: 149 us -> 137 us (0.919)
  Pallas kernels: 142 us -> 136 us
  local copies, waits for them, and re-layouts: 5.87 us -> 0 us
    pallas_call x1 -> x2, Pallas kernels: 142 us -> 136 us  [the longest x1 132 us: local_stack(): res = call(x, up[0], down[0], g)[:4]]
    unnamed x10 -> x0, local copies, waits for them, and re-layouts: 5.87 us -> none
where the time goes in v2:
time: 137 us; the launch traced here: 136 us
  Pallas kernels  136 us (99%)
    pallas_call x1, Pallas kernels, local_stack(): res = call(x, up[0], down[0], g)[:4]  132 us
    pallas_call x1, Pallas kernels, local_stack(): pl.pallas_call(copy_out, out_shape=[shape(q.shape, q.dtype) for q in res]...  3.43 us

profile of v2, /device:TPU:1, one launch (start us, length us, event | category | flops | bytes accessed | tf_op | source)
XLA Modules:
  0.0 136.4 jit_solution(9301296532856726866)
XLA Ops:
  0.6 132.2 %stack.1 = (bf16[1024,1024]{1,0:T(8,128)(2,1)}, bf16[1024,1024]{1,0:T(8,128)(2,1)}, f32[8,4096]{1,0:T(8,128)}, f32[32,1024]{1,0:T(8,128)}, f32[4,1024,256]{2,1,0:T(8,128)}, /*index=5*/f32[8,1024,256]{2,1,0:T(8,128)}) custom-call(bf16[1024,1024]{1,0:T(8,128)(2,1)} %xh.1, bf16[8,4096]{1,0:T(8,128)(2,1)} %bitcast.4, bf16[32,1024]{1,0:T(8,128)(2,1)} %bitcast.5, ...), custom_call_target="tpu_custom_call" | custom-call | tf_op jit(solution)/shard_map/stack/pallas_call | solution.py:643
  132.8 3.4 %copy_out.1 = (bf16[1024,1024]{1,0:T(8,128)(2,1)}, bf16[1024,1024]{1,0:T(8,128)(2,1)}, f32[8,4096]{1,0:T(8,128)}, f32[32,1024]{1,0:T(8,128)}) custom-call(bf16[1024,1024]{1,0:T(8,128)(2,1)} %get-tuple-element.12.refs_0_, bf16[1024,1024]{1,0:T(8,128)(2,1)} %get-tuple-element.13.refs_1_, f32[8,4096]{1,0:T(8,128)} %get-tuple-element.14.refs_2_, ...), custom_call_target="tpu_custom_call" | custom-call | tf_op jit(solution)/shard_map/copy_out/pallas_call | solution.py:644

commit v3 on v2

--- a/solution.py
+++ b/solution.py
@@ -22,8 +22,11 @@
 STEP = 512
 STEPS = 2 * TOK // STEP
 U2 = 16
-SLOTS = 4
+SLOTS = (4, 5, 5)
+FEW = 3
+SENDS = 4
 ROUNDS = (11, 11, 10)
+SHORT = 10
 CLASSES = DIMS = range(3)
 PAIRS = ((0, 1), (2,))
 BOTH = range(2)
@@ -135,9 +138,32 @@
                 self.wait(0, step, 0, i, 3)
 
 
+PLAN = (
+    ("end", 2, 11, 11007233111),
+    ("second_end", 1, 9, 11013252111),
+    ("middle", 1, 6, 11113051400),
+    ("end", 0, 3, 12114012511),
+    ("mid", 0, 1, 11211311303),
+    ("start", 0, 0, 10112221211),
+)
+
+
+def slots_of(first, later):
+    out = [first]
+    for digit in str(later)[1:]:
+        out.append(out[-1] + int(digit))
+    return out
+
+
+PLAN = [(name, ph, slots_of(*when)) for name, ph, *when in PLAN]
+LAST_SLOT = max(q for *_, slots in PLAN for q in slots)
+GIVE_SLOTS = (13, 15, 17, 18)
+TAKE_SLOTS = (20, 21, 22, 23)
+
+
 class Scatter:
-    def __init__(self, pc, pool, recv, sems, finish):
-        self.pc, self.pool, self.recv, self.sems, self.finish = pc, pool, recv, sems, finish
+    def __init__(self, pc, pool, recv, sems, credit, finish):
+        self.pc, self.pool, self.recv, self.sems, self.credit, self.finish = pc, pool, recv, sems, credit, finish
 
     @staticmethod
     def place_of(u):
@@ -157,15 +183,16 @@
             idx[free[0]] = part(half)
         return self.pool.at[(self.place_of(u), *idx)]
 
-    def landing(self, k, ph, slot, dirn, kind, half):
-        r = self.recv[ph][kind].at[k, slot, dirn]
+    def landing(self, n, k, ph, dirn, kind, half):
+        r = self.recv[ph][kind]
+        r = r.at[k, lax.rem(n, r.shape[1]), dirn]
         return r if half is None or not kind else r.at[part(half)]
 
     def ssem(self, n, pair, ph):
-        return self.sems[0].at[(ph * 2 + pair) * SLOTS + lax.rem(n, SLOTS)]
+        return self.sems[0].at[(ph * 2 + pair) * SENDS + lax.rem(n, SENDS)]
 
     def rsem(self, n, pair, ph, kind):
-        return self.sems[1].at[((ph * 2 + pair) * 2 + kind) * SLOTS + lax.rem(n, SLOTS)]
+        return self.sems[1].at[4 * sum(SLOTS[:ph]) + (pair * 2 + kind) * SLOTS[ph] + lax.rem(n, SLOTS[ph])]
 
     def send(self, n, k, ph, src, dst, kind, v):
         pair = k // 2
@@ -176,11 +203,30 @@
         near = self.pc.near(d, dirn)
         half = 1 - dirn if kind == 1 else dirn
         src = self.blk(n * 3 + k, k, ph, near if kind else self.pc.opp[d], half)
-        dst = self.landing(k, ph, lax.rem(n, SLOTS), dirn, min(kind, 1), half)
+        dst = self.landing(n, k, ph, dirn, min(kind, 1), half)
         self.send(n, k, ph, src, dst, min(kind, 1), near)
 
+    def start_short(self, n, ks):
+        slot = lax.rem(n, SLOTS[1])
+        for k in ks:
+            slots = [self.recv[1][1].at[k, slot, i] for i in BOTH] + [self.recv[3][0].at[k]]
+            for v, dst in zip(self.pc.others(ORDERS[k][1]), slots):
+                self.send(n, k, 1, self.blk(n * 3 + k, k, 1, v, None), dst, 1, v)
+
+    def end_short(self, n, ks):
+        slot = lax.rem(n, SLOTS[1])
+        arrived(self.recv[1][1].at[:, slot], self.rsem(n, 0, 1, 1))
+        for k in ks:
+            own = self.blk(n * 3 + k, k, 1, self.pc.c[ORDERS[k][1]], None)
+            tot = own[...] + self.recv[3][0].at[k][...]
+            for i in BOTH:
+                tot = tot + self.recv[1][1].at[k, slot, i][...]
+            own[...] = tot
+        self.sent(n, 0, 1)
+        self.start_last(n, ks)
+
     def received(self, n, pair, ph, kind):
-        r, slot = self.recv[ph][kind], lax.rem(n, SLOTS)
+        r, slot = self.recv[ph][kind], 0
         arrived(r.at[2, slot] if pair else r.at[pl.ds(0, 2), slot], self.rsem(n, pair, ph, kind))
 
     def sent(self, n, pair, ph):
@@ -192,15 +238,44 @@
         arrived(ref, self.ssem(n, pair, ph))
 
     def start(self, n, ks, ph):
+        if ph == 0:
+
+            @pl.when(n >= FEW)
+            def _():
+                for k in ks:
+                    for dirn in BOTH:
+                        pl.semaphore_wait(self.credit.at[2 * k + dirn], 1)
+
         for kind in BOTH:
             for k in ks:
                 for dirn in BOTH:
                     self.copy(n, k, ph, dirn, kind)
 
+    def give_credit(self, ks):
+        for k in ks:
+            d = ORDERS[k][0]
+            for dirn in BOTH:
+                to = self.pc.dev(d, self.pc.near(d, dirn))
+                pl.semaphore_signal(self.credit.at[2 * k + 1 - dirn], inc=1, device_id=to, device_id_type=MESH)
+
     def start_last(self, n, ks):
         for k in ks:
             for i, v in enumerate(self.pc.others(ORDERS[k][2])):
-                self.send(n, k, 2, self.blk(n * 3 + k, k, 2, v, None), self.recv[2][1].at[k, lax.rem(n, SLOTS), i], 1, v)
+                self.send(n, k, 2, self.blk(n * 3 + k, k, 2, v, None), self.recv[2][1].at[k, lax.rem(n, SLOTS[2]), i], 1, v)
+
+    @staticmethod
+    def choose(n, ks, usual, short):
+        if len(ks) == 1:
+            usual()
+        else:
+            pl.when(n < SHORT)(usual)
+            pl.when(n >= SHORT)(short)
+
+    def middle(self, n, ks, ph):
+        self.choose(n, ks, lambda: self.mid(n, ks, ph), lambda: None)
+
+    def second_end(self, n, ks, ph):
+        self.choose(n, ks, lambda: self.end(n, ks, ph), lambda: self.end_short(n, ks))
 
     def mid(self, n, ks, ph):
         self.received(n, ks[0] // 2, ph, 0)
@@ -208,10 +283,12 @@
             d = ORDERS[k][ph]
             for dirn in BOTH:
                 b = self.blk(n * 3 + k, k, ph, self.pc.near(d, dirn), dirn)
-                b[...] = b[...] + self.landing(k, ph, lax.rem(n, SLOTS), dirn, 0, None)[...]
+                b[...] = b[...] + self.landing(n, k, ph, dirn, 0, None)[...]
         for k in ks:
             for dirn in BOTH:
                 self.copy(n, k, ph, dirn, 2)
+        if ph == 0:
+            pl.when(n == 0)(lambda: self.give_credit(ks))
 
     def end(self, n, ks, ph):
         self.received(n, ks[0] // 2, ph, 1)
@@ -219,33 +296,35 @@
             own = self.blk(n * 3 + k, k, ph, self.pc.c[ORDERS[k][ph]], None)
             tot = own[...]
             for i in range(3 if ph == 2 else 2):
-                tot = tot + self.recv[ph][1].at[k, lax.rem(n, SLOTS), i][...]
+                tot = tot + self.recv[ph][1].at[k, lax.rem(n, SLOTS[ph]), i][...]
             if ph < 2:
                 own[...] = tot
             else:
                 self.finish(n * 3 + k, tot)
         self.sent(n, ks[0] // 2, ph)
         if ph == 0:
-            self.start(n, ks, 1)
+            self.choose(n, ks, lambda: self.start(n, ks, 1), lambda: self.start_short(n, ks))
+
+            pl.when(n + SLOTS[0] < ROUNDS[ks[0]])(lambda: self.give_credit(ks))
         elif ph == 1:
             self.start_last(n, ks)
 
-    def each(self, n, fn):
-        for ks in PAIRS:
-
-            @pl.when((n >= 0) & (n < ROUNDS[ks[0]]))
-            def _():
-                fn(n, ks)
-
-    def events(self, t):
-        self.each(t - 5, lambda n, ks: self.end(n, ks, 2))
-        for ph in (1, 0):
-            self.each(t - 2 - 2 * ph, lambda n, ks: self.end(n, ks, ph))
-            self.each(t - 1 - 2 * ph, lambda n, ks: self.mid(n, ks, ph))
-        self.begin(t + 1)
-
-    def begin(self, n):
-        self.each(n, lambda n, ks: self.start(n, ks, 0))
+    def events(self, t, come):
+        out = []
+        for (name, ph, slots), first in zip(PLAN, come):
+
+            def step(n, _):
+                for ks in PAIRS:
+
+                    @pl.when(n < ROUNDS[ks[0]])
+                    def _():
+                        getattr(self, name)(n, ks, ph)
+
+                return 0
+
+            out.append(sum(jnp.where(t >= q, 1, 0) for q in slots))
+            lax.fori_loop(first, out[-1], step, 0)
+        return tuple(out)
 
 
 def half_tanh(h, h2):
@@ -264,32 +343,31 @@
 
 def recv_shapes():
     out = []
-    for dims in ((R, R), (R,)):
+    for ph, dims in enumerate(((R, R), (R,))):
         for q in ((2, *dims[1:]), dims):
-            out.append((3, SLOTS, 2, *q, SUBL, COL))
-    return out + [(3, SLOTS, 3, SUBL, COL)]
+            out.append((3, SLOTS[ph] if ph or q == dims else FEW, 2, *q, SUBL, COL))
+    return out + [(3, SLOTS[2], 3, SUBL, COL), (2, R, SUBL, COL)]
 
 
 AG1, AG2 = Gather.count(W1_LANES), Gather.count(W2_LANES)
-RS_SEMS = 3 * 2 * SLOTS
 BLOCKS = DIM // COL
 
 
-def kernel(xh, uph, dnh, gh, yo, gxo, dw1o, dw2o, landh, keeph, x, xt, g, w1, w2, a, pool, sb, dw1s, dw1l, *rest):
-    recv, (ag_s, ag_r, rs_s, rs_r, lsem, xs, xr, spare_sem) = rest[:5], rest[5:]
+def kernel(xh, uph, dnh, gh, y, gx, dw1o, dw2o, landh, keeph, xp, xt, gp, w1, w2, a, pool, sb, dw1s, *rest):
+    recv, (ag_s, ag_r, rs_s, rs_r, lsem, xs, xr, spare_sem, credit) = rest[:6], rest[6:]
     pc = Place()
     s = pc.s
-    own, theirs = span(s, TOK), span(1 - s, TOK)
     my_lanes, their_lanes = span(s, HALF), span(1 - s, HALF)
     scope = jax.named_scope
+    tokens_x, tokens_g = (y, xp), (gx, gp)
 
     loads = [
         pltpu.make_async_copy(src, dst, lsem.at[i])
         for i, (src, dst) in enumerate((
             (uph.at[:, my_lanes], w1.at[(s, *pc.c)]),
             (dnh, w2.at[tuple(pc.c)]),
-            (xh, x.at[own]),
-            (gh, g.at[own]),
+            (xh, y),
+            (gh, gx),
         ))
     ]
     for c in loads:
@@ -306,8 +384,8 @@
         remote(src, dst, xs.at[i], xr.at[i], pc.partner)
         for i, (src, dst) in enumerate((
             (uph.at[:, their_lanes], w1.at[(s, *pc.c)]),
-            (xh, x.at[own]),
-            (gh, g.at[own]),
+            (xh, xp),
+            (gh, gp),
         ))
     ]
     for c in swaps:
@@ -349,23 +427,26 @@
     g2.start(2)
 
     def turn(i, _):
-        at = span(i, COL)
-        xt[:, at] = x[at, :].T
+        for q, part_x in enumerate(tokens_x):
+            xt[:, pl.ds(pl.multiple_of(q * TOK + i * COL, COL), COL)] = part_x[span(i, COL), :].T
         return 0
 
     loads[2].wait()
     swaps[1].wait_recv()
     with scope("turn"):
-        lax.fori_loop(0, 2 * TOK // COL, turn, 0)
+        lax.fori_loop(0, TOK // COL, turn, 0)
 
     def rows(i):
         return slice(STEP * i, STEP * (i + 1))
 
+    def step_of(pair, i):
+        return pair[i // 2][rows(i % 2), :]
+
     def flat(c, i):
         return units.at[R * c + i]
 
     def hidden_dot(c, i):
-        sb[i % 2, :STEP] = dot(x[rows(i), :], w1f[:, span(c, COL)], NN)
+        sb[i % 2, :STEP] = dot(step_of(tokens_x, i), w1f[:, span(c, COL)], NN)
 
     def hidden_act(c, i):
         h = sb[i % 2, :STEP]
@@ -373,7 +454,7 @@
         a[rows(i), span(c, COL)] = gelu(h).astype(bf16)
 
     def dhidden_dot(c, i):
-        sb[i % 2, :STEP] = dot(g[rows(i), :], w2f[span(c, COL), :], NT)
+        sb[i % 2, :STEP] = dot(step_of(tokens_g, i), w2f[span(c, COL), :], NT)
 
     def dhidden_act(c, i):
         slope = gelu_slope(flat(c, i)[...].reshape(STEP, COL))
@@ -393,30 +474,26 @@
             act_step(c, i)
 
     def grad2_rows(c, nb):
-        r = dot(a[:, span(c, COL)], g[:, pl.ds(nb * 2 * COL, 2 * COL)], TN)
+        cols = pl.ds(nb * 2 * COL, 2 * COL)
+        both = jnp.concatenate([q[:, cols] for q in tokens_g])
+        r = dot(a[:, span(c, COL)], both, TN)
         for b in BOTH:
             rr = r[:, COL * b:COL * (b + 1)].reshape(SUBL, R, SUBL, COL)
             for q in range(R):
                 units[2 * U2 + R * (2 * nb + b) + q, span(c, SUBL)] = rr[:, q]
 
-    def grad2(nb):
-        def body(i, _):
-            for q in range(R):
-                grad2_rows(i * R + q, nb)
-            return 0
-
-        lax.fori_loop(0, CHUNKS // R, body, 0)
+    def grad2_half(i, nb):
+        for q in range(R):
+            grad2_rows(i * R + q, nb)
+
+    own, theirs = pl.ds(0, TOK), pl.ds(TOK, TOK)
 
     def product(at, nb, i):
         lanes = span(nb, COL)
         return dot(a[at, :], w1f[lanes, :], NT) if i else dot(a[at, :], w2f[:, lanes], NN)
 
-    def out_block(nb, i):
-        lanes = span(nb, COL)
-        return pltpu.make_async_copy((x, g)[i].at[own, lanes], (yo, gxo)[i].at[:, lanes], lsem.at[R + BLOCKS * i + nb])
-
     def keep_y(n):
-        return pltpu.make_async_copy(sb.at[lax.rem(n, 3)], keeph.at[n], lsem.at[12 + lax.rem(n, 3)])
+        return pltpu.make_async_copy(sb.at[lax.rem(n, 3)], keeph.at[n], lsem.at[R + lax.rem(n, 3)])
 
     def give_y_block(nb):
         return remote(keeph.at[2 * nb], landh.at[nb], xs.at[3 + nb], xr.at[3 + nb], pc.partner)
@@ -433,16 +510,16 @@
         def _():
             kept(n - 3)
 
-        at = pl.ds(pl.multiple_of(TOK * jnp.where(lax.rem(n, 2) == 0, 1 - s, s), TOK), TOK)
+        at = span(1 - lax.rem(n, 2), TOK)
         sb[lax.rem(n, 3)] = product(at, lax.div(n, 2), 0)
         keep_y(n).start()
 
-    def finish_block(nb, i, at, part_sum):
-        res, lanes = (x, g)[i], span(nb, COL)
+    def finish_block(nb, res, at, part_sum):
+        lanes = span(nb, COL)
         res[at, lanes] = (res[at, lanes].astype(f32) + part_sum).astype(bf16)
 
     def fetched_y(nb):
-        return [pltpu.make_async_copy(src, sb.at[b], lsem.at[12 + b]) for b, src in enumerate((landh.at[nb], keeph.at[2 * nb + 1]))]
+        return [pltpu.make_async_copy(src, sb.at[b], lsem.at[R + b]) for b, src in enumerate((landh.at[nb], keeph.at[2 * nb + 1]))]
 
     def fetch_y(nb):
         give_y_block(nb).wait_recv()
@@ -454,12 +531,10 @@
             c.wait()
 
         def add(h, _):
-            at = pl.ds(pl.multiple_of(TOK * s + COL * h, COL), COL)
-            finish_block(nb, 0, at, sb[0, span(h, COL)] + sb[1, span(h, COL)])
+            finish_block(nb, y, span(h, COL), sb[0, span(h, COL)] + sb[1, span(h, COL)])
             return 0
 
         lax.fori_loop(0, TOK // COL, add, 0)
-        out_block(nb, 0).start()
 
     def spare(n):
         return units.at[pl.ds(R * n + 2, 2)]
@@ -475,12 +550,11 @@
         give_gx_block(nb).wait_recv()
 
         def add(h, _):
-            at = pl.ds(pl.multiple_of(TOK * s + STEP * h, STEP), STEP)
-            finish_block(nb, 1, at, product(at, nb, 1) + flat(nb, 2 + h)[...].reshape(STEP, COL))
+            at = span(h, STEP)
+            finish_block(nb, gx, at, product(at, nb, 1) + flat(nb, 2 + h)[...].reshape(STEP, COL))
             return 0
 
         lax.fori_loop(0, TOK // STEP, add, 0)
-        out_block(nb, 1).start()
 
     def loop(n, fn):
         def body(i, _):
@@ -532,9 +606,17 @@
         @pl.when(u >= U2)
         def _():
             v = u - U2
-            dw1s[lax.rem(v, 2), :, span(lax.div(v, 2), COL)] = tot
-
-    rs = Scatter(pc, pool, [recv[:2], recv[2:4], (None, recv[4])], (rs_s, rs_r), finish)
+            q = lax.div(v, 2)
+
+            @pl.when(lax.rem(v, 2) == s)
+            def _():
+                dw1o[:, pl.ds(pl.multiple_of(HALF * s + COL * q, COL), COL)] = tot
+
+            @pl.when(lax.rem(v, 2) != s)
+            def _():
+                dw1s[:, span(q, COL)] = tot
+
+    rs = Scatter(pc, pool, [recv[:2], recv[2:4], (None, recv[4]), recv[5:]], (rs_s, rs_r), credit, finish)
 
     def first_dot():
         for n in range(3):
@@ -550,103 +632,75 @@
         g1.drain()
         g2.drain()
 
-    def chunks_before(t):
-        return jnp.clip(2 * (t - 3), 0, CHUNKS)
-
-    with scope("start"):
-        rs.begin(jnp.int32(0))
-
-    def slot(t, _):
+    def slot(t, come):
         with scope("ev"):
-            rs.events(t)
-
-        at(t, 0, lambda: grad2(1))
-        at(t, 0, settle)
-        at(t, 1, lambda: loop(BLOCKS, lambda i: give_y(BLOCKS * (t - 1) + i)), 2)
-        at(t, 3, first_dot)
-
-        def more(c, _):
-            with scope("dh"):
-                dhidden(c)
-            return 0
-
-        lax.fori_loop(chunks_before(t), chunks_before(t + 1), more, 0)
-        at(t, 5, lambda: pl.semaphore_signal(spare_sem, inc=1, device_id=pc.partner, device_id_type=MESH))
-        at(t, 7, lambda: pl.semaphore_wait(spare_sem, 1))
+            come = rs.events(t, come)
+
+        at(t, 0, lambda: loop(2, lambda i: grad2_half(i, 1)))
+        at(t, 1, settle)
+        at(t, 1, lambda: loop(2, lambda i: give_y(2 * (t - 1) + i)), 4)
+        at(t, 5, first_dot)
+        at(t, 5, lambda: dhidden(t - 5), 12)
+        at(t, 9, lambda: pl.semaphore_signal(spare_sem, inc=1, device_id=pc.partner, device_id_type=MESH))
+        at(t, GIVE_SLOTS[0], lambda: pl.semaphore_wait(spare_sem, 1))
 
         def tokens(nb):
             fetch_y(nb)
             give_gx(nb)
             take_y(nb)
 
-        at(t, 7, lambda: loop(2, lambda i: tokens(2 * (t - 7) + i)), 8)
-        at(t, 9, lambda: take_gx(t - 9), 12)
-        return 0
-
-    lax.fori_loop(0, max(ROUNDS) + 5, slot, 0)
+        for slots, task in ((GIVE_SLOTS, tokens), (TAKE_SLOTS, take_gx)):
+            done = sum(jnp.where(t > q, 1, 0) for q in slots)
+            lax.fori_loop(done, sum(jnp.where(t >= q, 1, 0) for q in slots), lambda nb, _, task=task: task(nb) or 0, 0)
+
+        return come
+
+    lax.fori_loop(0, LAST_SLOT + 1, slot, (jnp.int32(0),) * len(PLAN))
 
     with scope("last"):
-        last = remote(dw1s.at[1 - s], dw1l, xs.at[11], xr.at[11], pc.partner)
+        last = remote(dw1s, dw1o.at[:, my_lanes], xs.at[11], xr.at[11], pc.partner)
         last.start()
-        dw1o[:, my_lanes] = dw1s[s]
         for c in swaps:
             c.wait_send()
         for nb in range(BLOCKS):
             give_y_block(nb).wait_send()
             give_gx_block(nb).wait_send()
-        for i in BOTH:
-            for nb in range(BLOCKS):
-                out_block(nb, i).wait()
         last.wait()
-        dw1o[:, their_lanes] = dw1l[...]
 
 
 def copy_out(*refs):
-    n = (len(refs) - 2) // 3
-    src, dst, mid, (into, out) = refs[:n], refs[n:2 * n], refs[2 * n:3 * n], refs[3 * n:]
-    pieces = []
-    for refs_of in zip(src, mid, dst):
-        rows = max(refs_of[0].shape[0] // 2, SUBL)
-        pieces += [[q.at[pl.ds(h, rows)] for q in refs_of] for h in range(0, refs_of[0].shape[0], rows)]
-    steps = [[pltpu.make_async_copy(p[e], p[e + 1], sem.at[i]) for e, sem in enumerate((into, out))] for i, p in enumerate(pieces)]
-    for first, _ in steps:
-        first.start()
-    for first, second in steps:
-        first.wait()
-        second.start()
-    for _, second in steps:
-        second.wait()
+    n = len(refs) // 2
+    copies = [pltpu.make_async_copy(src, dst, refs[-1].at[i]) for i, (src, dst) in enumerate(zip(refs[:n], refs[n:]))]
+    for c in copies:
+        c.start()
+    for c in copies:
+        c.wait()
 
 
 def local_stack(x, up, down, g):
     shape = jax.ShapeDtypeStruct
     dma = pltpu.SemaphoreType.DMA
-    bf = [(2 * TOK, DIM), (DIM, 2 * TOK), (2 * TOK, DIM), (2, R, R, R, SUBL, HALF), (R, R, R, HALF // R**3, DIM), (2 * TOK, HALF)]
-    ff = [(3 * U2, R, R, R, SUBL, COL), (3, TOK, COL), (2, SUBL, HALF), (SUBL, HALF)] + recv_shapes()
-    call = pl.pallas_call(
+    bf = [(TOK, DIM), (DIM, 2 * TOK), (TOK, DIM), (2, R, R, R, SUBL, HALF), (R, R, R, HALF // R**3, DIM), (2 * TOK, HALF)]
+    ff = [(3 * U2, R, R, R, SUBL, COL), (3, TOK, COL), (SUBL, HALF)] + recv_shapes()
+    results = [(x.shape, bf16), (g.shape, bf16), (up.shape[1:], f32), (down.shape[1:], f32)]
+    res = pl.pallas_call(
         kernel,
-        out_shape=(
-            shape(x.shape, bf16),
-            shape(g.shape, bf16),
-            shape(up.shape[1:], f32),
-            shape(down.shape[1:], f32),
-            shape((BLOCKS, TOK, COL), f32),
-            shape((2 * BLOCKS, TOK, COL), f32),
-        ),
+        out_shape=[pltpu.VMEM(*q) for q in results] + [shape((n, TOK, COL), f32) for n in (BLOCKS, 2 * BLOCKS)],
         in_specs=[ANY] * 4,
-        out_specs=(ANY, ANY, VMEM, VMEM, ANY, ANY),
+        out_specs=[VMEM] * 4 + [ANY] * 2,
         scratch_shapes=[pltpu.VMEM(q, bf16) for q in bf] + [pltpu.VMEM(q, f32) for q in ff]
-        + [dma((n,)) for n in (AG1 + AG2, AG1 + AG2, RS_SEMS, 2 * RS_SEMS, 15, 12, 12)] + [pltpu.SemaphoreType.REGULAR],
-        compiler_params=pltpu.CompilerParams(collective_id=0, has_side_effects=True, vmem_limit_bytes=67043328),
+        + [dma((n,)) for n in (AG1 + AG2, AG1 + AG2, 6 * SENDS, 4 * sum(SLOTS), 7, 12, 12)]
+        + [pltpu.SemaphoreType.REGULAR, pltpu.SemaphoreType.REGULAR((6,))],
+        compiler_params=pltpu.CompilerParams(collective_id=0, has_side_effects=True, vmem_limit_bytes=62586880),
         name="stack",
-    )
-    res = call(x, up[0], down[0], g)[:4]
+    )(x, up[0], down[0], g)[:4]
     y, gx, dw1, dw2 = pl.pallas_call(
         copy_out,
-        out_shape=[shape(q.shape, q.dtype) for q in res],
-        in_specs=[ANY] * 4,
+        out_shape=[shape(*q) for q in results],
+        in_specs=[VMEM] * 4,
         out_specs=[ANY] * 4,
-        scratch_shapes=[pltpu.VMEM(q.shape, q.dtype) for q in res] + [dma((2 * 4,))] * 2,
+        scratch_shapes=[dma((4,))],
+        compiler_params=pltpu.CompilerParams(vmem_limit_bytes=2**23),
         name="copy_out",
     )(*res)
     return y, gx, dw1[None], dw2[None]

time: 137 us -> 126 us (0.920)
  Pallas kernels: 136 us -> 125 us
    pallas_call x2, Pallas kernels: 136 us -> 125 us  [the longest x1 123 us: local_stack(): pl.pallas_call(kernel, out_shape=[pltpu.VMEM(*q) for q in results] + [sha...]
where the time goes in v3:
time: 126 us
  Pallas kernels  125 us (99%)
    pallas_call x1, Pallas kernels, local_stack(): pl.pallas_call(kernel, out_shape=[pltpu.VMEM(*q) for q in results] + [sha...  123 us

profile of v3, /device:TPU:1, one launch (start us, length us, event | category | flops | bytes accessed | tf_op | source)
XLA Modules:
  0.0 125.7 jit_solution(14677884648561077432)
XLA Ops:
  0.6 122.8 %stack.1 = (bf16[1024,1024]{1,0:T(8,128)(2,1)S(1)}, bf16[1024,1024]{1,0:T(8,128)(2,1)S(1)}, f32[8,4096]{1,0:T(8,128)S(1)}, f32[32,1024]{1,0:T(8,128)S(1)}, f32[4...) custom-call(bf16[1024,1024]{1,0:T(8,128)(2,1)} %xh.1, bf16[8,4096]{1,0:T(8,128)(2,1)} %bitcast.4, bf16[32,1024]{1,0:T(8,128)(2,1)} %bitcast.5, ...), custom_call_target="tpu_custom_call" | custom-call | tf_op jit(solution)/shard_map/stack/pallas_call | solution.py:686
  123.4 2.1 %copy_out.1 = (bf16[1024,1024]{1,0:T(8,128)(2,1)}, bf16[1024,1024]{1,0:T(8,128)(2,1)}, f32[8,4096]{1,0:T(8,128)}, f32[32,1024]{1,0:T(8,128)}) custom-call(bf16[1024,1024]{1,0:T(8,128)(2,1)S(1)} %get-tuple-element.12.refs_0_, bf16[1024,1024]{1,0:T(8,128)(2,1)S(1)} %get-tuple-element.13.refs_1_, f32[8,4096]{1,0:T(8,128)S(1)} %get-tuple-element.14.refs_2_, ...), custom_call_target="tpu_custom_call" | custom-call | tf_op jit(solution)/shard_map/copy_out/pallas_call | solution.py:697

commit v4 on v3

--- a/solution.py
+++ b/solution.py
@@ -16,7 +16,7 @@
 DIM = 1024
 HALF = 2048
 R = 4
-SUBL = 8
+SUBL, LANES = 8, 128
 COL = 256
 CHUNKS = HALF // COL
 STEP = 512
@@ -37,7 +37,7 @@
 ALL = slice(None)
 
 W1_LANES = ((0, COL, 3), (3 * COL, COL, 3), (6 * COL, COL, 2))
-W2_LANES = ((0, 256, 1), (256, 384, 1), (640, 384, 1))
+W2_LANES = ((0, LANES, 2), (2 * LANES, LANES, 3), (5 * LANES, LANES, 3))
 
 
 def dot(a, b, dims):
@@ -78,12 +78,14 @@
 
 
 class Gather:
+    OWN, EARLY, RING, PLANE, HALVES = range(5)
+
     def __init__(self, pc, w, lead, lanes, sems, base):
         self.pc, self.w, self.lead, self.lanes, self.sems, self.base = pc, w, lead, lanes, sems, base
 
     @staticmethod
     def count(lanes):
-        return 1 + 3 * max(n for _, _, n in lanes)
+        return 2 + 3 * max(n for _, _, n in lanes)
 
     def at(self, ln, changes):
         idx = list(self.pc.c)
@@ -96,56 +98,64 @@
 
     def stretch(self, k, step, i):
         lane0, width, subs = self.lanes[k]
-        return pl.ds(lane0 + i * width, width) if step else pl.ds(lane0, width * subs)
+        return pl.ds(lane0, width * subs) if step < self.RING else pl.ds(lane0 + i * width, width)
 
     def sem(self, q, step, i):
-        return self.sems[q].at[self.base + (3 * i + step if step else 0)]
-
-    def send(self, block, step, halves, i, d, v):
-        remote(block, block, self.sem(0, step, i), self.sem(1, step + halves, i), self.pc.dev(d, v)).start()
+        return self.sems[q].at[self.base + step + 3 * i]
+
+    def send(self, block, step, into, i, d, v):
+        remote(block, block, self.sem(0, step, i), self.sem(1, into, i), self.pc.dev(d, v)).start()
 
     def start(self, step, i=0):
         for k in self.classes(i):
-            block = self.at(self.stretch(k, step, i), [(d, ALL) for d in ORDERS[k][:step]])
-            d = ORDERS[k][step]
-            for v in self.pc.others(d)[:3 if step < 2 else 2]:
-                self.send(block, step, 0, i, d, v)
+            ln = self.stretch(k, step, i)
+            d1, d2, d3 = ORDERS[k]
+            d = (d1, d2, d2, d3)[step]
+            if step < self.RING:
+                blocks = [self.at(ln, ())]
+            elif step == self.RING:
+                blocks = [self.at(ln, ((d1, v),)) for v in self.pc.others(d1)]
+            else:
+                blocks = [self.at(ln, ((d1, ALL), (d2, ALL)))]
+            for v in self.pc.others(d)[:3 if step < self.PLANE else 2]:
+                for block in blocks:
+                    self.send(block, step, step, i, d, v)
 
     def mid(self, i=0):
-        self.wait(1, 2, 0, i, 2)
+        self.wait(1, self.PLANE, (2, R, R), i)
         for k in self.classes(i):
             d1, d2, d = ORDERS[k]
             for dirn in BOTH:
                 behind = self.pc.near(d, 1 - dirn)
-                block = self.at(self.stretch(k, 2, i), ((d1, part(dirn)), (d2, ALL), (d, behind)))
-                self.send(block, 2, 1, i, d, self.pc.near(d, dirn))
-
-    def wait(self, q, step, halves, i, n):
-        lanes = sum(self.lanes[k][1] * (1 if step else self.lanes[k][2]) for k in self.classes(i))
-        box = [pl.ds(0, m) for m in (n, *[R] * step, *[1] * (2 - step))]
-        arrived(self.w.at[(*self.lead, *box, ALL, pl.ds(0, lanes))], self.sem(q, step + halves, i))
+                block = self.at(self.stretch(k, self.PLANE, i), ((d1, part(dirn)), (d2, ALL), (d, behind)))
+                self.send(block, self.PLANE, self.HALVES, i, d, self.pc.near(d, dirn))
+
+    def wait(self, q, step, box, i):
+        lanes = sum(self.lanes[k][1] * (1 if step > self.EARLY else self.lanes[k][2]) for k in self.classes(i))
+        arrived(self.w.at[(*self.lead, *[pl.ds(0, m) for m in box], ALL, pl.ds(0, lanes))], self.sem(q, step, i))
 
     def end(self, step, i=0):
-        if step < 2:
-            self.wait(1, step, 0, i, 3)
-        else:
-            self.wait(1, step, 1, i, 1)
+        self.wait(1, step, ((3, 1, 1), (3, 1, 1), (3, 3, 1), None, (1, R, R))[step], i)
 
     def drain(self):
-        self.wait(0, 0, 0, 0, 3)
+        for step in (self.OWN, self.EARLY):
+            self.wait(0, step, (3, 1, 1), 0)
         for i in range(max(n for _, _, n in self.lanes)):
-            for step in (1, 2):
-                self.wait(0, step, 0, i, 3)
+            self.wait(0, self.RING, (3, 3, 1), i)
+            self.wait(0, self.PLANE, (3, R, R), i)
 
 
 PLAN = (
-    ("end", 2, 11, 11007233111),
-    ("second_end", 1, 9, 11013252111),
-    ("middle", 1, 6, 11113051400),
-    ("end", 0, 3, 12114012511),
-    ("mid", 0, 1, 11211311303),
-    ("start", 0, 0, 10112221211),
+    ("end", 2, 11, 11107363011),
+    ("second_end", 1, 9, 11013454310),
+    ("middle", 1, 6, 11113162313),
+    ("end", 0, 3, 12113122521),
+    ("mid", 0, 1, 11211312133),
+    ("start", 0, 0, 10112221212),
 )
+GIVE_SLOTS = (13, 15, 17, 18)
+TAKE_SLOTS = (20, 22, 24, 26)
+FIELD = 16
 
 
 def slots_of(first, later):
@@ -155,10 +165,16 @@
     return out
 
 
+def how_many(slots, t):
+    words = [sum(slots.count(FIELD * i + q) << (2 * q) for q in range(FIELD)) for i in range(LAST_SLOT // FIELD + 1)]
+    word = jnp.int32(0)
+    for i, value in enumerate(words):
+        word = jnp.where(lax.div(t, FIELD) == i, jnp.int32(value - (value >> 31 << 32)), word)
+    return lax.shift_right_logical(word, 2 * lax.rem(t, FIELD)) & 3
+
+
 PLAN = [(name, ph, slots_of(*when)) for name, ph, *when in PLAN]
 LAST_SLOT = max(q for *_, slots in PLAN for q in slots)
-GIVE_SLOTS = (13, 15, 17, 18)
-TAKE_SLOTS = (20, 21, 22, 23)
 
 
 class Scatter:
@@ -315,14 +331,11 @@
 
             def step(n, _):
                 for ks in PAIRS:
-
-                    @pl.when(n < ROUNDS[ks[0]])
-                    def _():
-                        getattr(self, name)(n, ks, ph)
-
+                    take = lambda: getattr(self, name)(n, ks, ph)
+                    pl.when(n < ROUNDS[ks[0]])(take) if ROUNDS[ks[0]] < max(ROUNDS) else take()
                 return 0
 
-            out.append(sum(jnp.where(t >= q, 1, 0) for q in slots))
+            out.append(first + how_many(slots, t))
             lax.fori_loop(first, out[-1], step, 0)
         return tuple(out)
 
@@ -401,31 +414,37 @@
     with scope("swapw"):
         loads[0].wait()
         swaps[0].wait_recv()
-    g1.start(0)
+    own, early, ring, plane, halves = range(5)
+    g1.start(own)
     loads[1].wait()
-    g2.start(0)
+    g2.start(own)
+    g1.start(early)
+    g2.start(early)
     with scope("own"):
-        g1.end(0)
+        g1.end(own)
     for i in range(3):
-        g1.start(1, i)
-    with scope("own2"):
-        g2.end(0)
-    g2.start(1)
+        g1.start(ring, i)
+    with scope("owntwo"):
+        g2.end(own)
+    for i in range(3):
+        g2.start(ring, i)
+    with scope("early"):
+        g1.end(early)
     for i in BOTH:
         with scope("ring"):
-            g1.end(1, i)
-        g1.start(2, i)
+            g1.end(ring, i)
+        g1.start(plane, i)
     with scope("mid"):
         g1.mid(0)
     with scope("ring"):
-        g1.end(1, 2)
-    g1.start(2, 2)
+        g1.end(ring, 2)
+    g1.start(plane, 2)
     with scope("mid"):
         g1.mid(1)
-    with scope("ring2"):
-        g2.end(1)
-    g2.start(2)
-
+    with scope("ringtwo"):
+        g2.end(early)
+        g2.end(ring, 0)
+    g2.start(plane, 0)
     def turn(i, _):
         for q, part_x in enumerate(tokens_x):
             xt[:, pl.ds(pl.multiple_of(q * TOK + i * COL, COL), COL)] = part_x[span(i, COL), :].T
@@ -454,20 +473,21 @@
         a[rows(i), span(c, COL)] = gelu(h).astype(bf16)
 
     def dhidden_dot(c, i):
-        sb[i % 2, :STEP] = dot(step_of(tokens_g, i), w2f[span(c, COL), :], NT)
+        sb[i] = dot(tokens_g[i][...], w2f[span(c, COL), :], NT)
 
     def dhidden_act(c, i):
-        slope = gelu_slope(flat(c, i)[...].reshape(STEP, COL))
-        a[rows(i), span(c, COL)] = (slope * sb[i % 2, :STEP]).astype(bf16)
+        for h in BOTH:
+            slope = gelu_slope(flat(c, 2 * i + h)[...].reshape(STEP, COL))
+            a[rows(2 * i + h), span(c, COL)] = (slope * sb[i, rows(h)]).astype(bf16)
 
     def grad1(c):
         r = dot(xt[...], a[:, span(c, COL)], NN)
         for p in BOTH:
             flat(c, p)[...] = r[rows(p)].reshape(STEP // SUBL, SUBL, COL)
 
-    def chunk_steps(dot_step, act_step, c, after):
-        for i in range(STEPS):
-            if i + 1 < STEPS:
+    def chunk_steps(steps, dot_step, act_step, c, after):
+        for i in range(steps):
+            if i + 1 < steps:
                 dot_step(c, i + 1)
             else:
                 dot_step(after, 0)
@@ -569,17 +589,29 @@
             with scope(f"task{first}"):
                 fn()
 
+    def last_sends():
+        g1.mid(2)
+        for i in (1, 2):
+            g2.end(ring, i)
+            g2.start(plane, i)
+
     def columns(i, _):
-        with scope("arrive"):
-            for q in range(3):
-                at(i, q, lambda q=q: g1.end(2, q))
-        at(i, 2, g2.mid)
         n = jnp.where(i < 2, 3, 2)
-        hidden_dot(i, 0)
 
         def step(q, _):
-            at(3 * i + q, 2, lambda: g1.mid(2))
-            chunk_steps(hidden_dot, hidden_act, i + 3 * q, i + 3 * jnp.minimum(q + 1, n - 1))
+            at(3 * i + q, 1, last_sends)
+            for sub, when in enumerate((3, 6, 6)):
+                at(3 * i + q, when, lambda: g2.mid(sub))
+            last = q == n - 1
+            for nxt in (1, 2):
+
+                @pl.when(last & (i + 1 == nxt))
+                def _():
+                    with scope("arrive"):
+                        g1.end(halves, nxt)
+
+            after = jnp.where(last, jnp.minimum(i + 1, CHUNKS - 6), i + 3 * q + 3)
+            chunk_steps(STEPS, hidden_dot, hidden_act, i + 3 * q, after)
             return 0
 
         with scope("hidden"):
@@ -594,6 +626,9 @@
 
         return 0
 
+    with scope("arrive"):
+        g1.end(halves, 0)
+    hidden_dot(0, 0)
     loads[3].wait()
     swaps[2].wait_recv()
     lax.fori_loop(0, 3, columns, 0)
@@ -624,17 +659,18 @@
         dhidden_dot(0, 0)
 
     def dhidden(c):
-        chunk_steps(dhidden_dot, dhidden_act, c, jnp.minimum(c + 1, CHUNKS - 1))
+        chunk_steps(2, dhidden_dot, dhidden_act, c, jnp.minimum(c + 1, CHUNKS - 1))
         grad1(c)
 
     def settle():
-        g2.end(2)
+        for i in range(3):
+            g2.end(halves, i)
         g1.drain()
         g2.drain()
 
     def slot(t, come):
         with scope("ev"):
-            come = rs.events(t, come)
+            come = (*rs.events(t, come[:-2]), *come[-2:])
 
         at(t, 0, lambda: loop(2, lambda i: grad2_half(i, 1)))
         at(t, 1, settle)
@@ -649,13 +685,13 @@
             give_gx(nb)
             take_y(nb)
 
-        for slots, task in ((GIVE_SLOTS, tokens), (TAKE_SLOTS, take_gx)):
-            done = sum(jnp.where(t > q, 1, 0) for q in slots)
-            lax.fori_loop(done, sum(jnp.where(t >= q, 1, 0) for q in slots), lambda nb, _, task=task: task(nb) or 0, 0)
-
-        return come
-
-    lax.fori_loop(0, LAST_SLOT + 1, slot, (jnp.int32(0),) * len(PLAN))
+        *come, given, taken = come
+        for slots, task, done in ((GIVE_SLOTS, tokens, given), (TAKE_SLOTS, take_gx, taken)):
+            come.append(done + how_many(slots, t))
+            pl.when(come[-1] > done)(lambda: task(done))
+        return tuple(come)
+
+    lax.fori_loop(0, LAST_SLOT + 1, slot, (jnp.int32(0),) * (len(PLAN) + 2))
 
     with scope("last"):
         last = remote(dw1s, dw1o.at[:, my_lanes], xs.at[11], xr.at[11], pc.partner)

time: 126 us -> 123 us (0.976)
  Pallas kernels: 125 us -> 122 us
    pallas_call x1, Pallas kernels: 123 us -> 119 us  [local_stack(): pl.pallas_call(kernel, out_shape=[pltpu.VMEM(*q) for q in results] + [sha...]
where the time goes in v4:
time: 123 us; the launch traced here: 122 us
  Pallas kernels  122 us (99%)
    pallas_call x1, Pallas kernels, local_stack(): pl.pallas_call(kernel, out_shape=[pltpu.VMEM(*q) for q in results] + [sha...  119 us

profile of v4, /device:TPU:1, one launch (start us, length us, event | category | flops | bytes accessed | tf_op | source)
XLA Modules:
  0.0 122.4 jit_solution(17853768013645541982)
XLA Ops:
  0.6 119.5 %stack.1 = (bf16[1024,1024]{1,0:T(8,128)(2,1)S(1)}, bf16[1024,1024]{1,0:T(8,128)(2,1)S(1)}, f32[8,4096]{1,0:T(8,128)S(1)}, f32[32,1024]{1,0:T(8,128)S(1)}, f32[4...) custom-call(bf16[1024,1024]{1,0:T(8,128)(2,1)} %xh.1, bf16[8,4096]{1,0:T(8,128)(2,1)} %bitcast.4, bf16[32,1024]{1,0:T(8,128)(2,1)} %bitcast.5, ...), custom_call_target="tpu_custom_call" | custom-call | tf_op jit(solution)/shard_map/stack/pallas_call | solution.py:722
  120.1 2.1 %copy_out.1 = (bf16[1024,1024]{1,0:T(8,128)(2,1)}, bf16[1024,1024]{1,0:T(8,128)(2,1)}, f32[8,4096]{1,0:T(8,128)}, f32[32,1024]{1,0:T(8,128)}) custom-call(bf16[1024,1024]{1,0:T(8,128)(2,1)S(1)} %get-tuple-element.12.refs_0_, bf16[1024,1024]{1,0:T(8,128)(2,1)S(1)} %get-tuple-element.13.refs_1_, f32[8,4096]{1,0:T(8,128)S(1)} %get-tuple-element.14.refs_2_, ...), custom_call_target="tpu_custom_call" | custom-call | tf_op jit(solution)/shard_map/copy_out/pallas_call | solution.py:733

commit v5 on v4

--- a/solution.py
+++ b/solution.py
@@ -21,6 +21,8 @@
 CHUNKS = HALF // COL
 STEP = 512
 STEPS = 2 * TOK // STEP
+DH_BUFFERS = (2, 0)
+Y_SLOT, DH_SLOT = 4, 8
 U2 = 16
 SLOTS = (4, 5, 5)
 FEW = 3
@@ -146,15 +148,15 @@
 
 
 PLAN = (
-    ("end", 2, 11, 11107363011),
-    ("second_end", 1, 9, 11013454310),
-    ("middle", 1, 6, 11113162313),
-    ("end", 0, 3, 12113122521),
-    ("mid", 0, 1, 11211312133),
-    ("start", 0, 0, 10112221212),
+    ("end", 2, 13, 13233233111),
+    ("second_end", 1, 11, 11232252201),
+    ("middle", 1, 9, 11221244202),
+    ("end", 0, 6, 12203213421),
+    ("mid", 0, 4, 11211312313),
+    ("start", 0, 2, 11112221221),
 )
-GIVE_SLOTS = (13, 15, 17, 18)
-TAKE_SLOTS = (20, 22, 24, 26)
+GIVE_SLOTS = (16, 18, 20, 21)
+TAKE_SLOTS = (22, 23, 25, 27)
 FIELD = 16
 
 
@@ -473,12 +475,12 @@
         a[rows(i), span(c, COL)] = gelu(h).astype(bf16)
 
     def dhidden_dot(c, i):
-        sb[i] = dot(tokens_g[i][...], w2f[span(c, COL), :], NT)
+        sb[DH_BUFFERS[i]] = dot(tokens_g[i][...], w2f[span(c, COL), :], NT)
 
     def dhidden_act(c, i):
         for h in BOTH:
             slope = gelu_slope(flat(c, 2 * i + h)[...].reshape(STEP, COL))
-            a[rows(2 * i + h), span(c, COL)] = (slope * sb[i, rows(h)]).astype(bf16)
+            a[rows(2 * i + h), span(c, COL)] = (slope * sb[DH_BUFFERS[i], rows(h)]).astype(bf16)
 
     def grad1(c):
         r = dot(xt[...], a[:, span(c, COL)], NN)
@@ -493,18 +495,12 @@
                 dot_step(after, 0)
             act_step(c, i)
 
-    def grad2_rows(c, nb):
-        cols = pl.ds(nb * 2 * COL, 2 * COL)
-        both = jnp.concatenate([q[:, cols] for q in tokens_g])
-        r = dot(a[:, span(c, COL)], both, TN)
-        for b in BOTH:
-            rr = r[:, COL * b:COL * (b + 1)].reshape(SUBL, R, SUBL, COL)
+    def grad2(b):
+        both = jnp.concatenate([q[:, span(b, COL)] for q in tokens_g])
+        for c in range(CHUNKS):
+            r = dot(a[:, COL * c:COL * (c + 1)], both, TN).reshape(SUBL, R, SUBL, COL)
             for q in range(R):
-                units[2 * U2 + R * (2 * nb + b) + q, span(c, SUBL)] = rr[:, q]
-
-    def grad2_half(i, nb):
-        for q in range(R):
-            grad2_rows(i * R + q, nb)
+                units[2 * U2 + R * b + q, SUBL * c:SUBL * (c + 1)] = r[:, q]
 
     own, theirs = pl.ds(0, TOK), pl.ds(TOK, TOK)
 
@@ -595,43 +591,24 @@
             g2.end(ring, i)
             g2.start(plane, i)
 
-    def columns(i, _):
-        n = jnp.where(i < 2, 3, 2)
-
-        def step(q, _):
-            at(3 * i + q, 1, last_sends)
-            for sub, when in enumerate((3, 6, 6)):
-                at(3 * i + q, when, lambda: g2.mid(sub))
-            last = q == n - 1
-            for nxt in (1, 2):
-
-                @pl.when(last & (i + 1 == nxt))
-                def _():
-                    with scope("arrive"):
-                        g1.end(halves, nxt)
-
-            after = jnp.where(last, jnp.minimum(i + 1, CHUNKS - 6), i + 3 * q + 3)
-            chunk_steps(STEPS, hidden_dot, hidden_act, i + 3 * q, after)
-            return 0
-
+    def chunk(q):
+        return lax.div(q, 3) + 3 * lax.rem(q, 3)
+
+    def hidden_step(q):
+        at(q, 2, last_sends)
+        at(q, 2, lambda: g1.end(halves, 1))
+        at(q, 4, lambda: g2.mid(0))
+        at(q, 5, lambda: g1.end(halves, 2))
+        at(q, 7, lambda: g2.mid(1))
         with scope("hidden"):
-            lax.fori_loop(0, n, step, 0)
-        with scope("gradtwo"):
-            for last in (1, 2):
-
-                @pl.when((i < 2) if last == 2 else (i == 2))
-                def _():
-                    for q in range(last + 1):
-                        grad2_rows(i + 3 * q, 0)
-
-        return 0
+            chunk_steps(STEPS, hidden_dot, hidden_act, chunk(q), chunk(jnp.minimum(q + 1, CHUNKS - 1)))
 
     with scope("arrive"):
         g1.end(halves, 0)
     hidden_dot(0, 0)
+    loop(CHUNKS, hidden_step)
     loads[3].wait()
     swaps[2].wait_recv()
-    lax.fori_loop(0, 3, columns, 0)
 
     def finish(u, tot):
         @pl.when(u < U2)
@@ -654,9 +631,9 @@
     rs = Scatter(pc, pool, [recv[:2], recv[2:4], (None, recv[4]), recv[5:]], (rs_s, rs_r), credit, finish)
 
     def first_dot():
-        for n in range(3):
-            kept(2 * BLOCKS - 3 + n)
+        kept(2 * BLOCKS - 3)
         dhidden_dot(0, 0)
+        kept(2 * BLOCKS - 2)
 
     def dhidden(c):
         chunk_steps(2, dhidden_dot, dhidden_act, c, jnp.minimum(c + 1, CHUNKS - 1))
@@ -672,12 +649,14 @@
         with scope("ev"):
             come = (*rs.events(t, come[:-2]), *come[-2:])
 
-        at(t, 0, lambda: loop(2, lambda i: grad2_half(i, 1)))
-        at(t, 1, settle)
-        at(t, 1, lambda: loop(2, lambda i: give_y(2 * (t - 1) + i)), 4)
-        at(t, 5, first_dot)
-        at(t, 5, lambda: dhidden(t - 5), 12)
-        at(t, 9, lambda: pl.semaphore_signal(spare_sem, inc=1, device_id=pc.partner, device_id_type=MESH))
+        at(t, 0, lambda: grad2(t), Y_SLOT - 1)
+        at(t, 0, lambda: g2.mid(2))
+        at(t, Y_SLOT, settle)
+        at(t, Y_SLOT, lambda: loop(2, lambda i: give_y(2 * (t - Y_SLOT) + i)), DH_SLOT - 1)
+        at(t, DH_SLOT, first_dot)
+        at(t, DH_SLOT, lambda: dhidden(t - DH_SLOT), DH_SLOT + CHUNKS - 1)
+        at(t, DH_SLOT + 1, lambda: kept(2 * BLOCKS - 1))
+        at(t, DH_SLOT + R, lambda: pl.semaphore_signal(spare_sem, inc=1, device_id=pc.partner, device_id_type=MESH))
         at(t, GIVE_SLOTS[0], lambda: pl.semaphore_wait(spare_sem, 1))
 
         def tokens(nb):

time: 123 us -> 122 us (level)
  no operation moved by 1% of the time
where the time goes in v5:
time: 122 us; the launch traced here: 121 us
  Pallas kernels  121 us (99%)
    pallas_call x1, Pallas kernels, local_stack(): pl.pallas_call(kernel, out_shape=[pltpu.VMEM(*q) for q in results] + [sha...  119 us

profile of v5, /device:TPU:1, one launch (start us, length us, event | category | flops | bytes accessed | tf_op | source)
XLA Modules:
  0.0 121.4 jit_solution(9858063308099389174)
XLA Ops:
  0.6 118.7 %stack.1 = (bf16[1024,1024]{1,0:T(8,128)(2,1)S(1)}, bf16[1024,1024]{1,0:T(8,128)(2,1)S(1)}, f32[8,4096]{1,0:T(8,128)S(1)}, f32[32,1024]{1,0:T(8,128)S(1)}, f32[4...) custom-call(bf16[1024,1024]{1,0:T(8,128)(2,1)} %xh.1, bf16[8,4096]{1,0:T(8,128)(2,1)} %bitcast.4, bf16[32,1024]{1,0:T(8,128)(2,1)} %bitcast.5, ...), custom_call_target="tpu_custom_call" | custom-call | tf_op jit(solution)/shard_map/stack/pallas_call | solution.py:701
  119.3 2.1 %copy_out.1 = (bf16[1024,1024]{1,0:T(8,128)(2,1)}, bf16[1024,1024]{1,0:T(8,128)(2,1)}, f32[8,4096]{1,0:T(8,128)}, f32[32,1024]{1,0:T(8,128)}) custom-call(bf16[1024,1024]{1,0:T(8,128)(2,1)S(1)} %get-tuple-element.12.refs_0_, bf16[1024,1024]{1,0:T(8,128)(2,1)S(1)} %get-tuple-element.13.refs_1_, f32[8,4096]{1,0:T(8,128)S(1)} %get-tuple-element.14.refs_2_, ...), custom_call_target="tpu_custom_call" | custom-call | tf_op jit(solution)/shard_map/copy_out/pallas_call | solution.py:712

commit v6 on v5

--- a/solution.py
+++ b/solution.py
@@ -642,8 +642,6 @@
     def settle():
         for i in range(3):
             g2.end(halves, i)
-        g1.drain()
-        g2.drain()
 
     def slot(t, come):
         with scope("ev"):
@@ -657,6 +655,8 @@
         at(t, DH_SLOT, lambda: dhidden(t - DH_SLOT), DH_SLOT + CHUNKS - 1)
         at(t, DH_SLOT + 1, lambda: kept(2 * BLOCKS - 1))
         at(t, DH_SLOT + R, lambda: pl.semaphore_signal(spare_sem, inc=1, device_id=pc.partner, device_id_type=MESH))
+        at(t, GIVE_SLOTS[0] + 1, g1.drain)
+        at(t, GIVE_SLOTS[0] + 1, g2.drain)
         at(t, GIVE_SLOTS[0], lambda: pl.semaphore_wait(spare_sem, 1))
 
         def tokens(nb):

time: 122 us -> 122 us (level)
  no operation moved by 1% of the time
where the time goes in v6:
time: 122 us; the launch traced here: 121 us
  Pallas kernels  121 us (99%)
    pallas_call x1, Pallas kernels, local_stack(): pl.pallas_call(kernel, out_shape=[pltpu.VMEM(*q) for q in results] + [sha...  119 us

profile of v6, /device:TPU:1, one launch (start us, length us, event | category | flops | bytes accessed | tf_op | source)
XLA Modules:
  0.0 121.4 jit_solution(11990180073694498916)
XLA Ops:
  0.6 118.7 %stack.1 = (bf16[1024,1024]{1,0:T(8,128)(2,1)S(1)}, bf16[1024,1024]{1,0:T(8,128)(2,1)S(1)}, f32[8,4096]{1,0:T(8,128)S(1)}, f32[32,1024]{1,0:T(8,128)S(1)}, f32[4...) custom-call(bf16[1024,1024]{1,0:T(8,128)(2,1)} %xh.1, bf16[8,4096]{1,0:T(8,128)(2,1)} %bitcast.4, bf16[32,1024]{1,0:T(8,128)(2,1)} %bitcast.5, ...), custom_call_target="tpu_custom_call" | custom-call | tf_op jit(solution)/shard_map/stack/pallas_call | solution.py:701
  119.3 2.1 %copy_out.1 = (bf16[1024,1024]{1,0:T(8,128)(2,1)}, bf16[1024,1024]{1,0:T(8,128)(2,1)}, f32[8,4096]{1,0:T(8,128)}, f32[32,1024]{1,0:T(8,128)}) custom-call(bf16[1024,1024]{1,0:T(8,128)(2,1)S(1)} %get-tuple-element.12.refs_0_, bf16[1024,1024]{1,0:T(8,128)(2,1)S(1)} %get-tuple-element.13.refs_1_, f32[8,4096]{1,0:T(8,128)S(1)} %get-tuple-element.14.refs_2_, ...), custom_call_target="tpu_custom_call" | custom-call | tf_op jit(solution)/shard_map/copy_out/pallas_call | solution.py:712
